TPU v7x, 32 devices: a whole 2x2x4 slice. The times are simulated.
32 devices in a mesh: vocab: 8 (over z, y), batch: 4 (over x, core).
Axes of the slice: x: 2, y: 2, z: 4, core: 2. Of those that a mesh axis runs over, the one named last changes fastest.
Arguments:
- tokens: bfloat16 [1024, 5120], P('batch'), may hold values from -180 to 180
- cluster_ids: int32 [1024, 1], P('batch'), may hold values from 0 to 3; in each aligned block of 256 rows (0 to 255, 256 to 511, ...) at most 128 rows name the same one
- head_weight: bfloat16 [5120, 4096], P('batch', 'vocab'), may hold values from -0.078125 to 0.078125
- cluster_weight: bfloat16 [5120, 4], replicated, may hold values from -0.078125 to 0.078125
- tail_proj: bfloat16 [5120, 2400], P('vocab'), may hold values from -0.078125 to 0.078125
- out_one: bfloat16 [1280, 4096], P(None, 'vocab'), may hold values from -0.15625 to 0.15625
- out_two: bfloat16 [640, 8192], P(None, 'vocab'), may hold values from -0.25 to 0.25
- out_three: bfloat16 [320, 8192], P(None, 'vocab'), may hold values from -0.3125 to 0.3125
- out_four: bfloat16 [160, 8192], P(None, 'vocab'), may hold values from -0.5 to 0.5
Outputs:
- head_logp: float32 [1024, 4096], P('batch', 'vocab')
- tail_one: float32 [512, 4096], P('batch', 'vocab')
- tail_two: float32 [512, 8192], P('batch', 'vocab')
- tail_three: float32 [512, 8192], P('batch', 'vocab')
- tail_four: float32 [512, 8192], P('batch', 'vocab')
Inputs may be any that keep to these rules, and one draw needn't show every extreme that they name: `cluster_ids`: in the 256 rows of one index of batch no cluster is named by more than 128 rows.
All inputs are finite; a program needn't handle non-finite values.
Results may differ from a plain program's by a relative error of at most 0.00057.
Values may be sent and summed in bfloat16 or wider, within the bound.
No kernel may reach another device: no remote copies, remote signals or barrier semaphores. Data moves between devices by JAX's collectives and lax.ppermute only.
A program may use at most 64 MiB of HBM per device.

v0:
```python
import functools

import jax
import jax.numpy as jnp
from jax import lax
from jax.experimental import pallas as pl
from jax.experimental.pallas import tpu as pltpu
from jax.sharding import PartitionSpec as P


CLUSTERS = 4
CAP = 128
LANES = 128
SUBLANES = 8
F32 = jnp.float32
BF16 = jnp.bfloat16


VMEM = pl.BlockSpec(memory_space=pltpu.VMEM)
SMEM = pl.BlockSpec(memory_space=pltpu.SMEM)
HBM = pl.BlockSpec(memory_space=pltpu.HBM)


def matmul(left, right):
    return jnp.dot(left, right, preferred_element_type=F32)


def iota(shape, axis):
    return lax.broadcasted_iota(jnp.int32, shape, axis)


def placement(ids):
    count = ids.shape[1]
    onehot = (ids == iota((SUBLANES, count), 0)).astype(F32)
    earlier = (iota((count, count), 0) < iota((count, count), 1)).astype(BF16)
    before = matmul(onehot.astype(BF16), earlier)
    slot = jnp.sum(before * onehot, axis=0, keepdims=True)
    counts = jnp.sum(onehot, axis=1, keepdims=True)
    first, second = counts[0:1], counts[1:2]
    filler = before[2:3] + before[3:4] + first
    filler = jnp.where(filler < CAP, filler, filler + second)
    row = jnp.where(ids == 0, slot, jnp.where(ids == 1, slot + CAP, filler))
    return slot.astype(jnp.int32), row.astype(jnp.int32), counts


def row_matrix(row):
    count = row.shape[1]
    return (row == iota((count, count), 0)).astype(BF16)


def contract_last(left, right):
    return lax.dot_general(left, right, (((1,), (1,)), ((), ())), preferred_element_type=F32)


def partial_kernel(widths, spread, me_ref, ids_ref, columns_ref, proj_ref, *refs):
    outs, (ids, columns, proj, total, sems) = refs[:-5], refs[-5:]
    one, two = widths[0], widths[1]
    rest = widths[2] + widths[3]
    features = columns.shape[1]
    if columns_ref.shape[1] == features:
        source = columns_ref
    else:
        source = columns_ref.at[:, pl.ds(pl.multiple_of(me_ref[0] * features, LANES), features)]
    ranges = ((one + two, rest), (0, one), (one, two))
    copies = [pltpu.make_async_copy(source, columns, sems.at[0])]
    first_copy = pltpu.make_async_copy(ids_ref, ids, sems.at[4])
    first_copy.start()
    for at, (begin, size) in enumerate(ranges):
        copies.append(
            pltpu.make_async_copy(
                proj_ref.at[pl.ds(begin, size), :], proj.at[pl.ds(begin, size), :], sems.at[1 + at]
            )
        )
    for copy in copies:
        copy.start()
    first_copy.wait()
    _, row, counts = placement(ids[...])
    matrix = row_matrix(row)
    copies[0].wait()
    rows = matmul(matrix, columns[...]).astype(BF16)
    upper, lower = rows[:CAP], rows[CAP:]
    number = iota((CAP, 1), 0).astype(F32)
    copies[1].wait()
    others = contract_last(rows, proj[one + two :])
    copies[2].wait()
    whole = contract_last(upper, proj[:one])
    total[:, rest:one] = whole[:, rest:]
    total[:, :rest] = jnp.where(number < counts[0:1], whole[:, :rest], others[:CAP])
    copies[3].wait()
    whole = contract_last(lower, proj[one : one + two])
    total[:, one + rest :] = whole[:, rest:]
    total[:, one : one + rest] = jnp.where(number < counts[1:2], whole[:, :rest], others[CAP:])
    if spread:
        chunk = outs[0].shape[0]
        for step, out in enumerate(outs):
            begin = pl.multiple_of((me_ref[0] ^ step) * chunk, chunk)
            out[...] = total[pl.ds(begin, chunk), :]
    else:
        outs[0][...] = total[...]


def unpack_kernel(ids_ref, pick_ref):
    ids = ids_ref[...]
    slot, row, _ = placement(ids)
    matrix = row_matrix(row)
    where = iota((CAP, ids.shape[1]), 0)
    for at, cluster in enumerate((2, 3)):
        own = ((ids == cluster) & (slot == where)).astype(BF16)
        pick_ref[at * CAP : (at + 1) * CAP, :] = contract_last(own, matrix).astype(BF16)


def pack_columns(columns):
    lane = iota((CAP, LANES), 1)
    square = jnp.zeros((CAP, LANES), F32)
    for at, column in enumerate(columns):
        square = jnp.where(lane == at, column, square)
    return square.T[:SUBLANES]


def row_stats(values):
    top = jnp.max(values, axis=1, keepdims=True)
    return top, jnp.sum(jnp.exp(values - top), axis=1, keepdims=True)


def head_more_kernel(steps, mine_ref, tokens_ref, *refs):
    weights, start, out = refs[:-2], refs[-2], refs[-1]
    total = start[...]
    for step, weight in zip(steps, weights):
        depth = weight.shape[0]
        begin = pl.multiple_of((mine_ref[0] ^ step) * depth, depth)
        total = total + matmul(tokens_ref[:, pl.ds(begin, depth)], weight[...])
    out[...] = total


def head_first_kernel(steps, mine_ref, tokens_ref, *refs):
    weights, out = refs[:-1], refs[-1]
    total = None
    for step, weight in zip(steps, weights):
        depth = weight.shape[0]
        begin = pl.multiple_of((mine_ref[0] ^ step) * depth, depth)
        part = matmul(tokens_ref[:, pl.ds(begin, depth)], weight[...])
        total = part if total is None else total + part
    out[...] = total


def head_last_kernel(steps, mine_ref, tokens_ref, *refs):
    weights, start, out, stats = refs[:-3], refs[-3], refs[-2], refs[-1]
    total = start[...]
    for step, weight in zip(steps, weights):
        depth = weight.shape[0]
        begin = pl.multiple_of((mine_ref[0] ^ step) * depth, depth)
        total = total + matmul(tokens_ref[:, pl.ds(begin, depth)], weight[...])
    out[...] = total
    top, mass = row_stats(total)
    stats[:SUBLANES] = pack_columns((top[:CAP], top[CAP:]))
    stats[SUBLANES:] = pack_columns((mass[:CAP], mass[CAP:]))


def score_kernel(widths, spread, me_ref, pick_ref, one_ref, two_ref, three_ref, four_ref, *refs):
    chunks = refs[:-6]
    scores, stats, joined = refs[-6:-2], refs[-2], refs[-1]
    if spread:
        chunk = chunks[0].shape[0]
        for step, ref in enumerate(chunks):
            begin = pl.multiple_of((me_ref[0] ^ step) * chunk, chunk)
            joined[pl.ds(begin, chunk), :] = ref[...]
    else:
        joined[...] = chunks[0][...]
    one, two = widths[0], widths[1]
    rest = widths[2] + widths[3]
    small = jnp.concatenate([joined[:, :rest], joined[:, one : one + rest]], axis=0)
    picked = matmul(pick_ref[...], small).astype(BF16)
    lefts = (
        joined[:, :one],
        joined[:, one : one + two],
        picked[:CAP, : widths[2]],
        picked[CAP:, widths[2] : rest],
    )
    tops, masses = [], []
    for left, weight, score in zip(lefts, (one_ref, two_ref, three_ref, four_ref), scores):
        value = matmul(left, weight[...])
        score[...] = value
        top, mass = row_stats(value)
        tops.append(top)
        masses.append(mass)
    zero = jnp.zeros((CAP, 1), F32)
    stats[:SUBLANES] = pack_columns([zero, zero] + tops)
    stats[SUBLANES:] = pack_columns([zero, zero] + masses)


def merge(own, other):
    top = jnp.maximum(own[:SUBLANES], other[:SUBLANES])
    mass = own[SUBLANES:] * jnp.exp(own[:SUBLANES] - top) + other[SUBLANES:] * jnp.exp(
        other[:SUBLANES] - top
    )
    return top, mass


def columns_of(rows):
    return jnp.concatenate([rows, jnp.zeros((LANES - SUBLANES, CAP), F32)], axis=0).T


def output_kernel(own_ref, other_ref, ids_ref, cluster_ref, head_ref, *refs):
    scores, head_out, outs = refs[:CLUSTERS], refs[CLUSTERS], refs[CLUSTERS + 1 :]
    ids = ids_ref[...]
    slot, _, counts = placement(ids)
    cluster_logits = cluster_ref[...]
    own_logit = jnp.sum(
        jnp.where(ids == iota(cluster_logits.shape, 0), cluster_logits, 0.0), axis=0, keepdims=True
    )
    top, mass = merge(own_ref[...], other_ref[...])
    head_top = jnp.concatenate([top[0:1], top[1:2]], axis=1)
    head_mass = jnp.concatenate([mass[0:1], mass[1:2]], axis=1)
    overall = jnp.maximum(head_top, jnp.max(cluster_logits, axis=0, keepdims=True))
    denominator = head_mass * jnp.exp(head_top - overall) + jnp.sum(
        jnp.exp(cluster_logits - overall), axis=0, keepdims=True
    )
    log_total = overall + jnp.log(denominator)
    number = iota((SUBLANES, CAP), 0)
    logs = jnp.where(
        number == 0, log_total[:, :CAP], jnp.where(number == 1, log_total[:, CAP:], top + jnp.log(mass))
    )
    columns = columns_of(logs)
    head_out[:CAP] = head_ref[:CAP] - columns[:, 0:1]
    head_out[CAP:] = head_ref[CAP:] - columns[:, 1:2]
    own_logp = own_logit - log_total
    here = slot == iota((CAP, ids.shape[1]), 0)
    number = iota((CAP, 1), 0).astype(F32)
    for cluster in range(CLUSTERS):
        slot_logp = jnp.sum(jnp.where((ids == cluster) & here, own_logp, 0.0), axis=1, keepdims=True)
        shift = columns[:, 2 + cluster : 3 + cluster] - slot_logp
        outs[cluster][...] = jnp.where(
            number < counts[cluster : cluster + 1], scores[cluster][...] - shift, 0.0
        )


def shapes(*pairs):
    return [jax.ShapeDtypeStruct(shape, kind) for shape, kind in pairs]


def in_hbm(value):
    return pltpu.with_memory_space_constraint(value, pltpu.HBM)


def limit(mebibytes):
    return pltpu.CompilerParams(vmem_limit_bytes=mebibytes * 2**20)


def cost(flops, size):
    return pl.CostEstimate(flops=int(flops), bytes_accessed=int(size), transcendentals=0)


def shards(
    sizes,
    tokens,
    cluster_ids,
    head_weight,
    cluster_weight,
    tail_proj,
    out_one,
    out_two,
    out_three,
    out_four,
):
    members, groups = sizes
    me = lax.axis_index("vocab")
    mine = lax.axis_index("batch")
    out_weights = (out_one, out_two, out_three, out_four)
    widths = tuple(weight.shape[0] for weight in out_weights)
    packed = widths[0] + widths[1]
    chunk = CAP // members
    spread = chunk % 16 == 0
    count = tokens.shape[0]

    def exchange(value, axis, size, step):
        return lax.ppermute(value, axis, [(at, at ^ step) for at in range(size)])

    features = tail_proj.shape[0]
    ids = cluster_ids.T
    if features % LANES:
        columns = lax.dynamic_slice_in_dim(tokens, me * features, features, 1)
    else:
        columns = tokens
    me_index = me.reshape(1).astype(jnp.int32)
    parts = pl.pallas_call(
        functools.partial(partial_kernel, widths, spread),
        out_shape=shapes(*([((chunk, packed), F32)] * members if spread else [((CAP, packed), F32)])),
        in_specs=[SMEM, HBM, HBM, HBM],
        out_specs=[VMEM] * (members if spread else 1),
        scratch_shapes=[
            pltpu.VMEM((1, count), jnp.int32),
            pltpu.VMEM((count, features), BF16),
            pltpu.VMEM(tail_proj.shape[::-1], BF16),
            pltpu.VMEM((CAP, packed), F32),
            pltpu.SemaphoreType.DMA((5,)),
        ],
        compiler_params=limit(8),
        cost_estimate=cost(2 * count * features * 2 * packed, 4 * features * packed),
        name="partial",
    )(me_index, in_hbm(ids), in_hbm(columns), in_hbm(tail_proj.T))
    if not spread:
        parts = [
            lax.dynamic_slice_in_dim(parts[0], (me ^ step) * chunk, chunk, 0) for step in range(members)
        ]
    parts, head_weight = lax.optimization_barrier((parts, head_weight))
    pairs = [
        parts[step] + exchange(parts[step + 1], "vocab", members, 1)
        for step in reversed(range(0, members, 2))
    ][::-1]
    arrived = [pairs[0]] + [exchange(pairs[at], "vocab", members, 2 * at) for at in reversed(range(1, members // 2))]

    steps = [step for step in range(0, groups, 2)]
    far = [exchange(head_weight, "batch", groups, step) for step in steps[1:]]
    near = exchange(head_weight, "batch", groups, 1)
    mine_index = mine.reshape(1).astype(jnp.int32)
    vocab = head_weight.shape[1]
    depth = head_weight.shape[0]
    head_start = pl.pallas_call(
        functools.partial(head_first_kernel, (0, 1)),
        out_shape=shapes(((count, vocab), F32))[0],
        in_specs=[SMEM, VMEM, VMEM, VMEM],
        out_specs=VMEM,
        compiler_params=limit(6),
        cost_estimate=cost(2 * count * vocab * depth * 2, depth * vocab * 4),
        name="head_first",
    )(mine_index, tokens, head_weight, near)
    pick = pl.pallas_call(
        unpack_kernel,
        out_shape=shapes(((2 * CAP, count), BF16))[0],
        in_specs=[VMEM],
        out_specs=VMEM,
        compiler_params=limit(2),
        cost_estimate=cost(2 * count * count * count * 2, 4 * count * count),
        name="unpack",
    )(ids)
    cluster_logits = lax.dot_general(
        cluster_weight, tokens, (((0,), (1,)), ((), ())), preferred_element_type=F32
    )
    arrived, head_start, cluster_logits = lax.optimization_barrier((arrived, head_start, cluster_logits))
    own = sum(arrived[1:], arrived[0]).astype(BF16)
    evens = [own] + [exchange(own, "vocab", members, step) for step in range(2, members, 2)]
    _, far = lax.optimization_barrier((evens[-1], far))
    chunks = []
    for value in evens:
        chunks += [value, exchange(value, "vocab", members, 1)]
    if not spread:
        stacked = jnp.stack(chunks)
        order = me ^ jnp.arange(members)
        chunks = [jnp.take(stacked, order, axis=0).reshape(CAP, packed)]

    rest = [exchange(value, "batch", groups, 1) for value in far]
    head_more = pl.pallas_call(
        functools.partial(head_more_kernel, tuple(steps[1:])),
        out_shape=shapes(((count, vocab), F32))[0],
        in_specs=[SMEM] + [VMEM] * (len(far) + 2),
        out_specs=VMEM,
        compiler_params=limit(6),
        cost_estimate=cost(2 * count * vocab * depth * len(far), depth * vocab * 4),
        name="head_more",
    )(mine_index, tokens, *far, head_start)
    head_logits, head_stats = pl.pallas_call(
        functools.partial(head_last_kernel, tuple(step ^ 1 for step in steps[1:])),
        out_shape=shapes(((count, vocab), F32), ((2 * SUBLANES, CAP), F32)),
        in_specs=[SMEM] + [VMEM] * (len(rest) + 2),
        out_specs=[VMEM] * 2,
        compiler_params=limit(6),
        cost_estimate=cost(2 * count * vocab * depth * len(rest), depth * vocab * 4),
        name="head_last",
    )(mine_index, tokens, *rest, head_more)
    score_shapes = [((CAP, weight.shape[1]), F32) for weight in out_weights]
    *scores, stats = pl.pallas_call(
        functools.partial(score_kernel, widths, spread),
        out_shape=shapes(*score_shapes, ((2 * SUBLANES, CAP), F32)),
        in_specs=[SMEM] + [VMEM] * (5 + len(chunks)),
        out_specs=[VMEM] * (CLUSTERS + 1),
        scratch_shapes=[pltpu.VMEM((CAP, packed), BF16)],
        compiler_params=limit(6),
        cost_estimate=cost(
            2 * CAP * sum(weight.size for weight in out_weights), 2 * sum(weight.size for weight in out_weights)
        ),
        name="scores",
    )(me_index, pick, *out_weights, *chunks)

    stats = jnp.where(lax.rem(iota(stats.shape, 0), SUBLANES) < 2, head_stats, stats)
    step = 1
    while 2 * step < members:
        stats = jnp.concatenate(merge(stats, exchange(stats, "vocab", members, step)), axis=0)
        step = 2 * step
    other = exchange(stats, "vocab", members, step)
    out_shapes = [((count, vocab), F32)] + score_shapes
    return tuple(
        pl.pallas_call(
            output_kernel,
            out_shape=shapes(*out_shapes),
            in_specs=[VMEM] * (5 + CLUSTERS),
            out_specs=[VMEM] * (1 + CLUSTERS),
            compiler_params=limit(6),
        cost_estimate=cost(count * vocab * 8, 8 * count * vocab * 8),
            name="outputs",
        )(stats, other, ids, cluster_logits, head_logits, *scores)
    )


def solution(mesh):
    in_specs = (
        P("batch", None),
        P("batch", None),
        P("batch", "vocab"),
        P(),
        P("vocab", None),
        P(None, "vocab"),
        P(None, "vocab"),
        P(None, "vocab"),
        P(None, "vocab"),
    )
    out_specs = (P("batch", "vocab"),) * 5
    sizes = (mesh.shape["vocab"], mesh.shape["batch"])

    def whole(*args):
        return shards(sizes, *args)

    return jax.shard_map(whole, mesh=mesh, in_specs=in_specs, out_specs=out_specs, check_vma=False)
```

profile of v0, /device:TPU:0, one launch (start us, length us, event | category | flops | bytes accessed | tf_op | source)
XLA Modules:
  0.0 64.9 jit_solution(9661534130078346654)
XLA Ops:
  0.7 3.1 %partial.1 = (f32[16,1920]{1,0:T(8,128)S(1)}, f32[16,1920]{1,0:T(8,128)S(1)}, f32[16,1920]{1,0:T(8,128)S(1)}, f32[16,1920]{1,0:T(8,128)S(1)}, f32[16,1920]{1,0:T...) custom-call(s32[1]{0:T(128)} %bitcast.1.me_ref, s32[1,256]{1,0:T(1,128)} %bitcast.6, ...), custom_call_target="tpu_custom_call" | custom-call | flops 1258291200 | bytes 4915200 | tf_op jit(solution)/shard_map/partial/pallas_call | solution.py:285
  3.8 0.6 collective-permute-start.7
  4.4 2.6 %collective-permute-start.9 = (bf16[1280,512]{1,0:T(8,128)(2,1)}, bf16[1280,512]{1,0:T(8,128)(2,1)}, u32[]{:S(2)}, u32[]{:S(2)}) collective-permute-start(bf16[1280,512]{1,0:T(8,128)(2,1)} %refs_0_), channel_id=1, source_target_pairs={{0,2},{1,3},{2,0},{3,1},{4,6},{5,7},{6,4},{7,5},{8,10},{9,11},{10,... | collective-permute-start | bytes 3932168 | tf_op jit(solution)/shard_map/ppermute | solution.py:276
  6.9 1.5 %collective-permute-start.1 = (f32[16,1920]{1,0:T(8,128)S(1)}, f32[16,1920]{1,0:T(8,128)S(1)}, u32[]{:S(2)}, u32[]{:S(2)}) collective-permute-start(f32[16,1920]{1,0:T(8,128)S(1)} %get-tuple-element.47), channel_id=1, source_target_pairs={{0,4},{4,0},{8,12},{12,8},{16,20},{20,16},{24,28},{28,24},{1,5},{5... | collective-permute-start | bytes 368648 | tf_op jit(solution)/shard_map/ppermute | solution.py:276
  9.0 1.5 %collective-permute-start.5 = (f32[16,1920]{1,0:T(8,128)S(1)}, f32[16,1920]{1,0:T(8,128)S(1)}, u32[]{:S(2)}, u32[]{:S(2)}) collective-permute-start(f32[16,1920]{1,0:T(8,128)S(1)} %get-tuple-element.51), channel_id=1, source_target_pairs={{0,4},{4,0},{8,12},{12,8},{16,20},{20,16},{24,28},{28,24},{1,5},{5... | collective-permute-start | bytes 368648 | tf_op jit(solution)/shard_map/ppermute | solution.py:276
  10.5 2.6 %collective-permute-done.1 = f32[16,1920]{1,0:T(8,128)S(1)} collective-permute-done((f32[16,1920]{1,0:T(8,128)S(1)}, f32[16,1920]{1,0:T(8,128)S(1)}, u32[]{:S(2)}, u32[]{:S(2)}) %collective-permute-start.1) | collective-permute-done | bytes 122912 | tf_op jit(solution)/shard_map/ppermute | solution.py:276
  13.1 1.5 %collective-permute-start = (f32[16,1920]{1,0:T(8,128)S(1)}, f32[16,1920]{1,0:T(8,128)S(1)}, u32[]{:S(2)}, u32[]{:S(2)}) collective-permute-start(f32[16,1920]{1,0:T(8,128)S(1)} %get-tuple-element.45), channel_id=1, source_target_pairs={{0,4},{4,0},{8,12},{12,8},{16,20},{20,16},{24,28},{28,24},{1,5},{5... | collective-permute-start | bytes 368648 | tf_op jit(solution)/shard_map/ppermute | solution.py:276
  14.7 1.1 %collective-permute-done.3 = f32[16,1920]{1,0:T(8,128)S(1)} collective-permute-done((f32[16,1920]{1,0:T(8,128)S(1)}, f32[16,1920]{1,0:T(8,128)S(1)}, u32[]{:S(2)}, u32[]{:S(2)}) %collective-permute-start.3) | collective-permute-done | bytes 122912 | tf_op jit(solution)/shard_map/ppermute | solution.py:276
  15.8 3.6 %collective-permute-start.2 = (f32[16,1920]{1,0:T(8,128)S(1)}, f32[16,1920]{1,0:T(8,128)S(1)}, u32[]{:S(2)}, u32[]{:S(2)}) collective-permute-start(f32[16,1920]{1,0:T(8,128)S(1)} %add.28), channel_id=1, source_target_pairs={{0,24},{4,28},{8,16},{12,20},{16,8},{20,12},{24,0},{28,4},{1,25},{... | collective-permute-start | bytes 368648 | tf_op jit(solution)/shard_map/ppermute | solution.py:276
  19.4 1.6 %collective-permute-start.4 = (f32[16,1920]{1,0:T(8,128)S(1)}, f32[16,1920]{1,0:T(8,128)S(1)}, u32[]{:S(2)}, u32[]{:S(2)}) collective-permute-start(f32[16,1920]{1,0:T(8,128)S(1)} %add.29), channel_id=1, source_target_pairs={{0,16},{4,20},{8,24},{12,28},{16,0},{20,4},{24,8},{28,12},{1,17},{... | collective-permute-start | bytes 368648 | tf_op jit(solution)/shard_map/ppermute | solution.py:276
  21.0 1.6 %collective-permute-start.6 = (f32[16,1920]{1,0:T(8,128)S(1)}, f32[16,1920]{1,0:T(8,128)}, u32[]{:S(2)}, u32[]{:S(2)}) collective-permute-start(f32[16,1920]{1,0:T(8,128)S(1)} %add.30), channel_id=1, source_target_pairs={{0,8},{4,12},{8,0},{12,4},{16,24},{20,28},{24,16},{28,20},{1,9},{5... | collective-permute-start | bytes 368648 | tf_op jit(solution)/shard_map/ppermute | solution.py:276
  22.7 0.8 %fusion.2.cluster_ref = f32[4,256]{1,0:T(4,128)S(1)} fusion(bf16[5120,4]{0,1:T(4,128)(2,1)S(1)} %copy-done, bf16[256,5120]{1,0:T(8,128)(2,1)S(1)} %copy-done.1), kind=kOutput, calls=%fused_computation.12 | convolution fusion | flops 10485760 | bytes 2666496 | tf_op jit(solution)/shard_map/dot_general | solution.py:336
  23.5 2.6 %head_first.1.refs_1_ = f32[256,512]{1,0:T(8,128)S(1)} custom-call(s32[1]{0:T(128)} %bitcast.mine_ref, bf16[256,5120]{1,0:T(8,128)(2,1)S(1)} %copy-done.1, bf16[1280,512]{1,0:T(8,128)(2,1)} %refs_0_, bf16[1280,512]{1,0:T(8,128)(2,1)} %collective-permute-done.7.refs_1_), custom_call_target="tpu_custom_call" | custom-call | flops 671088640 | bytes 2621440 | tf_op jit(solution)/shard_map/head_first/pallas_call | solution.py:318
  26.1 2.4 %collective-permute-done.4 = f32[16,1920]{1,0:T(8,128)S(1)} collective-permute-done((f32[16,1920]{1,0:T(8,128)S(1)}, f32[16,1920]{1,0:T(8,128)S(1)}, u32[]{:S(2)}, u32[]{:S(2)}) %collective-permute-start.4) | collective-permute-done | bytes 122912 | tf_op jit(solution)/shard_map/ppermute | solution.py:276
  28.5 0.9 %add_convert_fusion.refs_0_ = bf16[16,1920]{1,0:T(8,128)(2,1)S(1)} fusion(f32[16,1920]{1,0:T(8,128)} %collective-permute-done.6, f32[16,1920]{1,0:T(8,128)S(1)} %collective-permute-done.4, f32[16,1920]{1,0:T(8,128)S(1)} %add.27, f32[16,1920]{1,0:T(8,128)S(1)} %collective-permute-done.2), kind=kLoop, calls=%fused_computation | loop fusion | flops 122880 | bytes 552960 | tf_op jit(solution)/shard_map/convert_element_type | solution.py:340
  29.4 3.5 %collective-permute-start.8 = (bf16[16,1920]{1,0:T(8,128)(2,1)S(1)}, bf16[16,1920]{1,0:T(8,128)(2,1)S(1)}, u32[]{:S(2)}, u32[]{:S(2)}) collective-permute-start(bf16[16,1920]{1,0:T(8,128)(2,1)S(1)} %add_convert_fusion.refs_0_), channel_id=1, source_target_pairs={{0,24},{4,28},{8,16},{12,20},{16,8},{20,12},{24,0},{28,4},{1,25},{... | collective-permute-start | bytes 184328 | tf_op jit(solution)/shard_map/ppermute | solution.py:276
  32.9 3.7 %collective-permute-done.9.refs_0_ = bf16[1280,512]{1,0:T(8,128)(2,1)} collective-permute-done((bf16[1280,512]{1,0:T(8,128)(2,1)}, bf16[1280,512]{1,0:T(8,128)(2,1)}, u32[]{:S(2)}, u32[]{:S(2)}) %collective-permute-start.9) | collective-permute-done | bytes 1310752 | tf_op jit(solution)/shard_map/ppermute | solution.py:276
  36.6 1.8 %collective-permute-start.12 = (bf16[16,1920]{1,0:T(8,128)(2,1)S(1)}, bf16[16,1920]{1,0:T(8,128)(2,1)S(1)}, u32[]{:S(2)}, u32[]{:S(2)}) collective-permute-start(bf16[16,1920]{1,0:T(8,128)(2,1)S(1)} %add_convert_fusion.refs_0_), channel_id=1, source_target_pairs={{0,8},{4,12},{8,0},{12,4},{16,24},{20,28},{24,16},{28,20},{1,9},{5... | collective-permute-start | bytes 184328 | tf_op jit(solution)/shard_map/ppermute | solution.py:276
  38.5 2.6 %collective-permute-start.14 = (bf16[16,1920]{1,0:T(8,128)(2,1)S(1)}, bf16[16,1920]{1,0:T(8,128)(2,1)S(1)}, u32[]{:S(2)}, u32[]{:S(2)}) collective-permute-start(bf16[16,1920]{1,0:T(8,128)(2,1)S(1)} %add_convert_fusion.refs_0_), channel_id=1, source_target_pairs={{0,16},{4,20},{8,24},{12,28},{16,0},{20,4},{24,8},{28,12},{1,17},{... | collective-permute-start | bytes 184328 | tf_op jit(solution)/shard_map/ppermute | solution.py:276
  41.0 1.5 %collective-permute-start.11 = (bf16[16,1920]{1,0:T(8,128)(2,1)S(1)}, bf16[16,1920]{1,0:T(8,128)(2,1)S(1)}, u32[]{:S(2)}, u32[]{:S(2)}) collective-permute-start(bf16[16,1920]{1,0:T(8,128)(2,1)S(1)} %add_convert_fusion.refs_0_), channel_id=1, source_target_pairs={{0,4},{4,0},{8,12},{12,8},{16,20},{20,16},{24,28},{28,24},{1,5},{5... | collective-permute-start | bytes 184328 | tf_op jit(solution)/shard_map/ppermute | solution.py:276
  43.1 1.5 %collective-permute-start.13 = (bf16[16,1920]{1,0:T(8,128)(2,1)S(1)}, bf16[16,1920]{1,0:T(8,128)(2,1)S(1)}, u32[]{:S(2)}, u32[]{:S(2)}) collective-permute-start(bf16[16,1920]{1,0:T(8,128)(2,1)S(1)} %collective-permute-done.12.refs_2_), channel_id=1, source_target_pairs={{0,4},{4,0},{8,12},{12,8},{16,20},{20,16},{24,28},{28,24},{1,5},{5... | collective-permute-start | bytes 184328 | tf_op jit(solution)/shard_map/ppermute | solution.py:276
  44.9 1.5 %collective-permute-start.15 = (bf16[16,1920]{1,0:T(8,128)(2,1)S(1)}, bf16[16,1920]{1,0:T(8,128)(2,1)S(1)}, u32[]{:S(2)}, u32[]{:S(2)}) collective-permute-start(bf16[16,1920]{1,0:T(8,128)(2,1)S(1)} %collective-permute-done.14.refs_4_), channel_id=1, source_target_pairs={{0,4},{4,0},{8,12},{12,8},{16,20},{20,16},{24,28},{28,24},{1,5},{5... | collective-permute-start | bytes 184328 | tf_op jit(solution)/shard_map/ppermute | solution.py:276
  46.8 2.0 %head_more.1.refs_1_ = f32[256,512]{1,0:T(8,128)S(1)} custom-call(s32[1]{0:T(128)} %bitcast.mine_ref, bf16[256,5120]{1,0:T(8,128)(2,1)S(1)} %copy-done.1, bf16[1280,512]{1,0:T(8,128)(2,1)} %collective-permute-done.9.refs_0_, f32[256,512]{1,0:T(8,128)S(1)} %head_first.1.refs_1_), custom_call_target="tpu_custom_call" | custom-call | flops 335544320 | bytes 2621440 | tf_op jit(solution)/shard_map/head_more/pallas_call | solution.py:352
  49.2 1.1 %scores.1 = (f32[128,512]{1,0:T(8,128)S(1)}, f32[128,1024]{1,0:T(8,128)S(1)}, f32[128,1024]{1,0:T(8,128)S(1)}, f32[128,1024]{1,0:T(8,128)S(1)}, f32[16,128]{1,0:T(8,128)S(1)}) custom-call(s32[1]{0:T(128)} %bitcast.1.me_ref, bf16[256,256]{1,0:T(8,128)(2,1)S(1)} %unpack.1.pick_ref, bf16[1280,512]{1,0:T(8,128)(2,1)S(1)} %copy-done.2, ...), custom_call_target="tpu_custom_call" | custom-call | flops 461373440 | bytes 3604480 | tf_op jit(solution)/shard_map/scores/pallas_call | solution.py:371
  50.4 0.7 %head_last.1 = (f32[256,512]{1,0:T(8,128)S(1)}, f32[16,128]{1,0:T(8,128)S(1)}) custom-call(s32[1]{0:T(128)} %bitcast.mine_ref, bf16[256,5120]{1,0:T(8,128)(2,1)S(1)} %copy-done.1, bf16[1280,512]{1,0:T(8,128)(2,1)S(1)} %collective-permute-done.10.refs_0_, f32[256,512]{1,0:T(8,128)S(1)} %head_more.1.refs_1_), custom_call_target="tpu_custom_call" | custom-call | flops 335544320 | bytes 2621440 | tf_op jit(solution)/shard_map/head_last/pallas_call | solution.py:361
  51.2 1.4 %collective-permute-start.17 = (f32[16,128]{1,0:T(8,128)S(1)}, f32[16,128]{1,0:T(8,128)S(1)}, u32[]{:S(2)}, u32[]{:S(2)}) collective-permute-start(f32[16,128]{1,0:T(8,128)S(1)} %broadcast_select_fusion), channel_id=1, source_target_pairs={{0,4},{4,0},{8,12},{12,8},{16,20},{20,16},{24,28},{28,24},{1,5},{5... | collective-permute-start | bytes 24584 | tf_op jit(solution)/shard_map/ppermute | solution.py:276
  52.6 2.3 %collective-permute-done.17 = f32[16,128]{1,0:T(8,128)S(1)} collective-permute-done((f32[16,128]{1,0:T(8,128)S(1)}, f32[16,128]{1,0:T(8,128)S(1)}, u32[]{:S(2)}, u32[]{:S(2)}) %collective-permute-start.17) | collective-permute-done | bytes 8224 | tf_op jit(solution)/shard_map/ppermute | solution.py:276
  54.9 0.5 collective-permute-start.18
  55.4 3.2 %collective-permute-done.18 = f32[16,128]{1,0:T(8,128)S(1)} collective-permute-done((f32[16,128]{1,0:T(8,128)S(1)}, f32[16,128]{1,0:T(8,128)S(1)}, u32[]{:S(2)}, u32[]{:S(2)}) %collective-permute-start.18) | collective-permute-done | bytes 8224 | tf_op jit(solution)/shard_map/ppermute | solution.py:276
  58.6 1.3 %collective-permute-start.19 = (f32[16,128]{1,0:T(8,128)S(1)}, f32[16,128]{1,0:T(8,128)S(1)}, u32[]{:S(2)}, u32[]{:S(2)}) collective-permute-start(f32[16,128]{1,0:T(8,128)S(1)} %pad_maximum_fusion.1.own_ref), channel_id=1, source_target_pairs={{0,16},{4,20},{8,24},{12,28},{16,0},{20,4},{24,8},{28,12},{1,17},{... | collective-permute-start | bytes 24584 | tf_op jit(solution)/shard_map/ppermute | solution.py:276
  59.9 3.3 %collective-permute-done.19.other_ref = f32[16,128]{1,0:T(8,128)S(1)} collective-permute-done((f32[16,128]{1,0:T(8,128)S(1)}, f32[16,128]{1,0:T(8,128)S(1)}, u32[]{:S(2)}, u32[]{:S(2)}) %collective-permute-start.19) | collective-permute-done | bytes 8224 | tf_op jit(solution)/shard_map/ppermute | solution.py:276
  63.2 1.7 %outputs.1 = (f32[256,512]{1,0:T(8,128)}, f32[128,512]{1,0:T(8,128)}, f32[128,1024]{1,0:T(8,128)}, f32[128,1024]{1,0:T(8,128)}, f32[128,1024]{1,0:T(8,128)}) custom-call(f32[16,128]{1,0:T(8,128)S(1)} %pad_maximum_fusion.1.own_ref, f32[16,128]{1,0:T(8,128)S(1)} %collective-permute-done.19.other_ref, s32[1,256]{1,0:T(1,128)S(1)} %bitcast.8, ...), custom_call_target="tpu_custom_call" | custom-call | flops 1048576 | bytes 8388608 | tf_op jit(solution)/shard_map/outputs/pallas_call | solution.py:392
  (41 shorter events, 2.3 us)
Async XLA Ops:
  0.6 22.0 %copy-start = (bf16[5120,4]{0,1:T(4,128)(2,1)S(1)}, bf16[5120,4]{0,1:T(4,128)(2,1)}, u32[]{:S(2)}) copy-start(bf16[5120,4]{0,1:T(4,128)(2,1)} %param.12) | copy-start | bytes 122884
  0.7 22.0 %copy-start.1 = (bf16[256,5120]{1,0:T(8,128)(2,1)S(1)}, bf16[256,5120]{1,0:T(8,128)(2,1)}, u32[]{:S(2)}) copy-start(bf16[256,5120]{1,0:T(8,128)(2,1)} %tokens_ref.5) | copy-start | bytes 7864324
  3.8 19.7 %collective-permute-start.7 = (bf16[1280,512]{1,0:T(8,128)(2,1)}, bf16[1280,512]{1,0:T(8,128)(2,1)}, u32[]{:S(2)}, u32[]{:S(2)}) collective-permute-start(bf16[1280,512]{1,0:T(8,128)(2,1)} %refs_0_), channel_id=1, source_target_pairs={{0,1},{1,0},{2,3},{3,2},{4,5},{5,4},{6,7},{7,6},{8,9},{9,8},{10,11... | collective-permute-start | bytes 3932168 | tf_op jit(solution)/shard_map/ppermute | solution.py:276
  4.4 32.2 %collective-permute-start.9 = (bf16[1280,512]{1,0:T(8,128)(2,1)}, bf16[1280,512]{1,0:T(8,128)(2,1)}, u32[]{:S(2)}, u32[]{:S(2)}) collective-permute-start(bf16[1280,512]{1,0:T(8,128)(2,1)} %refs_0_), channel_id=1, source_target_pairs={{0,2},{1,3},{2,0},{3,1},{4,6},{5,7},{6,4},{7,5},{8,10},{9,11},{10,... | collective-permute-start | bytes 3932168 | tf_op jit(solution)/shard_map/ppermute | solution.py:276
  6.9 6.2 %collective-permute-start.1 = (f32[16,1920]{1,0:T(8,128)S(1)}, f32[16,1920]{1,0:T(8,128)S(1)}, u32[]{:S(2)}, u32[]{:S(2)}) collective-permute-start(f32[16,1920]{1,0:T(8,128)S(1)} %get-tuple-element.47), channel_id=1, source_target_pairs={{0,4},{4,0},{8,12},{12,8},{16,20},{20,16},{24,28},{28,24},{1,5},{5... | collective-permute-start | bytes 368648 | tf_op jit(solution)/shard_map/ppermute | solution.py:276
  8.4 7.3 %collective-permute-start.3 = (f32[16,1920]{1,0:T(8,128)S(1)}, f32[16,1920]{1,0:T(8,128)S(1)}, u32[]{:S(2)}, u32[]{:S(2)}) collective-permute-start(f32[16,1920]{1,0:T(8,128)S(1)} %get-tuple-element.49), channel_id=1, source_target_pairs={{0,4},{4,0},{8,12},{12,8},{16,20},{20,16},{24,28},{28,24},{1,5},{5... | collective-permute-start | bytes 368648 | tf_op jit(solution)/shard_map/ppermute | solution.py:276
  9.0 10.4 %collective-permute-start.5 = (f32[16,1920]{1,0:T(8,128)S(1)}, f32[16,1920]{1,0:T(8,128)S(1)}, u32[]{:S(2)}, u32[]{:S(2)}) collective-permute-start(f32[16,1920]{1,0:T(8,128)S(1)} %get-tuple-element.51), channel_id=1, source_target_pairs={{0,4},{4,0},{8,12},{12,8},{16,20},{20,16},{24,28},{28,24},{1,5},{5... | collective-permute-start | bytes 368648 | tf_op jit(solution)/shard_map/ppermute | solution.py:276
  13.1 7.9 %collective-permute-start = (f32[16,1920]{1,0:T(8,128)S(1)}, f32[16,1920]{1,0:T(8,128)S(1)}, u32[]{:S(2)}, u32[]{:S(2)}) collective-permute-start(f32[16,1920]{1,0:T(8,128)S(1)} %get-tuple-element.45), channel_id=1, source_target_pairs={{0,4},{4,0},{8,12},{12,8},{16,20},{20,16},{24,28},{28,24},{1,5},{5... | collective-permute-start | bytes 368648 | tf_op jit(solution)/shard_map/ppermute | solution.py:276
  15.8 10.3 %collective-permute-start.2 = (f32[16,1920]{1,0:T(8,128)S(1)}, f32[16,1920]{1,0:T(8,128)S(1)}, u32[]{:S(2)}, u32[]{:S(2)}) collective-permute-start(f32[16,1920]{1,0:T(8,128)S(1)} %add.28), channel_id=1, source_target_pairs={{0,24},{4,28},{8,16},{12,20},{16,8},{20,12},{24,0},{28,4},{1,25},{... | collective-permute-start | bytes 368648 | tf_op jit(solution)/shard_map/ppermute | solution.py:276
  19.4 9.1 %collective-permute-start.4 = (f32[16,1920]{1,0:T(8,128)S(1)}, f32[16,1920]{1,0:T(8,128)S(1)}, u32[]{:S(2)}, u32[]{:S(2)}) collective-permute-start(f32[16,1920]{1,0:T(8,128)S(1)} %add.29), channel_id=1, source_target_pairs={{0,16},{4,20},{8,24},{12,28},{16,0},{20,4},{24,8},{28,12},{1,17},{... | collective-permute-start | bytes 368648 | tf_op jit(solution)/shard_map/ppermute | solution.py:276
  21.0 7.5 %collective-permute-start.6 = (f32[16,1920]{1,0:T(8,128)S(1)}, f32[16,1920]{1,0:T(8,128)}, u32[]{:S(2)}, u32[]{:S(2)}) collective-permute-start(f32[16,1920]{1,0:T(8,128)S(1)} %add.30), channel_id=1, source_target_pairs={{0,8},{4,12},{8,0},{12,4},{16,24},{20,28},{24,16},{28,20},{1,9},{5... | collective-permute-start | bytes 368648 | tf_op jit(solution)/shard_map/ppermute | solution.py:276
  23.5 22.9 %copy-start.6 = (s32[256,1]{0,1:T(1,128)S(1)}, s32[256,1]{0,1:T(1,128)}, u32[]{:S(2)}) copy-start(s32[256,1]{0,1:T(1,128)} %param.10) | copy-start | bytes 3076
  29.4 7.2 %collective-permute-start.8 = (bf16[16,1920]{1,0:T(8,128)(2,1)S(1)}, bf16[16,1920]{1,0:T(8,128)(2,1)S(1)}, u32[]{:S(2)}, u32[]{:S(2)}) collective-permute-start(bf16[16,1920]{1,0:T(8,128)(2,1)S(1)} %add_convert_fusion.refs_0_), channel_id=1, source_target_pairs={{0,24},{4,28},{8,16},{12,20},{16,8},{20,12},{24,0},{28,4},{1,25},{... | collective-permute-start | bytes 184328 | tf_op jit(solution)/shard_map/ppermute | solution.py:276
  36.6 13.8 %collective-permute-start.10 = (bf16[1280,512]{1,0:T(8,128)(2,1)}, bf16[1280,512]{1,0:T(8,128)(2,1)S(1)}, u32[]{:S(2)}, u32[]{:S(2)}) collective-permute-start(bf16[1280,512]{1,0:T(8,128)(2,1)} %collective-permute-done.9.refs_0_), channel_id=1, source_target_pairs={{0,1},{1,0},{2,3},{3,2},{4,5},{5,4},{6,7},{7,6},{8,9},{9,8},{10,11... | collective-permute-start | bytes 3932168 | tf_op jit(solution)/shard_map/ppermute | solution.py:276
  36.6 6.4 %collective-permute-start.12 = (bf16[16,1920]{1,0:T(8,128)(2,1)S(1)}, bf16[16,1920]{1,0:T(8,128)(2,1)S(1)}, u32[]{:S(2)}, u32[]{:S(2)}) collective-permute-start(bf16[16,1920]{1,0:T(8,128)(2,1)S(1)} %add_convert_fusion.refs_0_), channel_id=1, source_target_pairs={{0,8},{4,12},{8,0},{12,4},{16,24},{20,28},{24,16},{28,20},{1,9},{5... | collective-permute-start | bytes 184328 | tf_op jit(solution)/shard_map/ppermute | solution.py:276
  38.5 6.4 %collective-permute-start.14 = (bf16[16,1920]{1,0:T(8,128)(2,1)S(1)}, bf16[16,1920]{1,0:T(8,128)(2,1)S(1)}, u32[]{:S(2)}, u32[]{:S(2)}) collective-permute-start(bf16[16,1920]{1,0:T(8,128)(2,1)S(1)} %add_convert_fusion.refs_0_), channel_id=1, source_target_pairs={{0,16},{4,20},{8,24},{12,28},{16,0},{20,4},{24,8},{28,12},{1,17},{... | collective-permute-start | bytes 184328 | tf_op jit(solution)/shard_map/ppermute | solution.py:276
  41.0 7.8 %collective-permute-start.11 = (bf16[16,1920]{1,0:T(8,128)(2,1)S(1)}, bf16[16,1920]{1,0:T(8,128)(2,1)S(1)}, u32[]{:S(2)}, u32[]{:S(2)}) collective-permute-start(bf16[16,1920]{1,0:T(8,128)(2,1)S(1)} %add_convert_fusion.refs_0_), channel_id=1, source_target_pairs={{0,4},{4,0},{8,12},{12,8},{16,20},{20,16},{24,28},{28,24},{1,5},{5... | collective-permute-start | bytes 184328 | tf_op jit(solution)/shard_map/ppermute | solution.py:276
  42.6 6.6 %collective-permute-start.16 = (bf16[16,1920]{1,0:T(8,128)(2,1)S(1)}, bf16[16,1920]{1,0:T(8,128)(2,1)S(1)}, u32[]{:S(2)}, u32[]{:S(2)}) collective-permute-start(bf16[16,1920]{1,0:T(8,128)(2,1)S(1)} %collective-permute-done.8.refs_6_), channel_id=1, source_target_pairs={{0,4},{4,0},{8,12},{12,8},{16,20},{20,16},{24,28},{28,24},{1,5},{5... | collective-permute-start | bytes 184328 | tf_op jit(solution)/shard_map/ppermute | solution.py:276
  43.1 5.8 %collective-permute-start.13 = (bf16[16,1920]{1,0:T(8,128)(2,1)S(1)}, bf16[16,1920]{1,0:T(8,128)(2,1)S(1)}, u32[]{:S(2)}, u32[]{:S(2)}) collective-permute-start(bf16[16,1920]{1,0:T(8,128)(2,1)S(1)} %collective-permute-done.12.refs_2_), channel_id=1, source_target_pairs={{0,4},{4,0},{8,12},{12,8},{16,20},{20,16},{24,28},{28,24},{1,5},{5... | collective-permute-start | bytes 184328 | tf_op jit(solution)/shard_map/ppermute | solution.py:276
  44.9 4.3 %collective-permute-start.15 = (bf16[16,1920]{1,0:T(8,128)(2,1)S(1)}, bf16[16,1920]{1,0:T(8,128)(2,1)S(1)}, u32[]{:S(2)}, u32[]{:S(2)}) collective-permute-start(bf16[16,1920]{1,0:T(8,128)(2,1)S(1)} %collective-permute-done.14.refs_4_), channel_id=1, source_target_pairs={{0,4},{4,0},{8,12},{12,8},{16,20},{20,16},{24,28},{28,24},{1,5},{5... | collective-permute-start | bytes 184328 | tf_op jit(solution)/shard_map/ppermute | solution.py:276
  46.8 2.4 %copy-start.2 = (bf16[1280,512]{1,0:T(8,128)(2,1)S(1)}, bf16[1280,512]{1,0:T(8,128)(2,1)}, u32[]{:S(2)}) copy-start(bf16[1280,512]{1,0:T(8,128)(2,1)} %one_ref.1) | copy-start | bytes 3932164
  46.8 2.4 %copy-start.3 = (bf16[640,1024]{1,0:T(8,128)(2,1)S(1)}, bf16[640,1024]{1,0:T(8,128)(2,1)}, u32[]{:S(2)}) copy-start(bf16[640,1024]{1,0:T(8,128)(2,1)} %two_ref.1) | copy-start | bytes 3932164
  46.8 2.4 %copy-start.4 = (bf16[320,1024]{1,0:T(8,128)(2,1)S(1)}, bf16[320,1024]{1,0:T(8,128)(2,1)}, u32[]{:S(2)}) copy-start(bf16[320,1024]{1,0:T(8,128)(2,1)} %three_ref.1) | copy-start | bytes 1966084
  46.8 2.4 %copy-start.5 = (bf16[160,1024]{1,0:T(8,128)(2,1)S(1)}, bf16[160,1024]{1,0:T(8,128)(2,1)}, u32[]{:S(2)}) copy-start(bf16[160,1024]{1,0:T(8,128)(2,1)} %four_ref.1) | copy-start | bytes 983044
  51.2 3.7 %collective-permute-start.17 = (f32[16,128]{1,0:T(8,128)S(1)}, f32[16,128]{1,0:T(8,128)S(1)}, u32[]{:S(2)}, u32[]{:S(2)}) collective-permute-start(f32[16,128]{1,0:T(8,128)S(1)} %broadcast_select_fusion), channel_id=1, source_target_pairs={{0,4},{4,0},{8,12},{12,8},{16,20},{20,16},{24,28},{28,24},{1,5},{5... | collective-permute-start | bytes 24584 | tf_op jit(solution)/shard_map/ppermute | solution.py:276
  54.9 3.7 %collective-permute-start.18 = (f32[16,128]{1,0:T(8,128)S(1)}, f32[16,128]{1,0:T(8,128)S(1)}, u32[]{:S(2)}, u32[]{:S(2)}) collective-permute-start(f32[16,128]{1,0:T(8,128)S(1)} %pad_maximum_fusion), channel_id=1, source_target_pairs={{0,8},{4,12},{8,0},{12,4},{16,24},{20,28},{24,16},{28,20},{1,9},{5... | collective-permute-start | bytes 24584 | tf_op jit(solution)/shard_map/ppermute | solution.py:276
  58.6 4.6 %collective-permute-start.19 = (f32[16,128]{1,0:T(8,128)S(1)}, f32[16,128]{1,0:T(8,128)S(1)}, u32[]{:S(2)}, u32[]{:S(2)}) collective-permute-start(f32[16,128]{1,0:T(8,128)S(1)} %pad_maximum_fusion.1.own_ref), channel_id=1, source_target_pairs={{0,16},{4,20},{8,24},{12,28},{16,0},{20,4},{24,8},{28,12},{1,17},{... | collective-permute-start | bytes 24584 | tf_op jit(solution)/shard_map/ppermute | solution.py:276
where the time goes:
time: 65.1 us; the launch traced here: 64.9 us
  starting transfers between devices  31.2 us (48%)
  waiting for transfers between devices  19.3 us (30%)
  Pallas kernels  11.6 us (18%)
  other arithmetic  1.12 us (2%)
  between operations  0.83 us (1%)
  matrix products  0.77 us (1%)
    ppermute x20, starting transfers between devices, exchange(): return lax.ppermute(value, axis, [(at, at ^ step) for at in range(size)])  31.2 us
    ppermute x20, waiting for transfers between devices, exchange(): return lax.ppermute(value, axis, [(at, at ^ step) for at in range(size)])  19.3 us
    pallas_call x1, Pallas kernels, shards(): pl.pallas_call(functools.partial(partial_kernel, widths, spread), out_sha...  3.15 us
    pallas_call x1, Pallas kernels, shards(): pl.pallas_call(functools.partial(head_first_kernel, (0, 1)), out_shape=sh...  2.56 us
    pallas_call x1, Pallas kernels, shards(): pl.pallas_call(functools.partial(head_more_kernel, tuple(steps[1:])), out...  1.97 us
    pallas_call x1, Pallas kernels, shards(): pl.pallas_call(output_kernel, out_shape=shapes(*out_shapes), in_specs=[VM...  1.69 us
  transfers between devices with their start and end apart: 20, of which 9 were waited for; matrix products, arithmetic and copies ran while one was open for 3% of the time, Pallas kernels for 9%

commit v1 on v0

--- a/solution.py
+++ b/solution.py
@@ -52,7 +52,7 @@
     return lax.dot_general(left, right, (((1,), (1,)), ((), ())), preferred_element_type=F32)
 
 
-def partial_kernel(widths, spread, me_ref, ids_ref, columns_ref, proj_ref, *refs):
+def partial_kernel(widths, spread, me_ref, mine_ref, ids_ref, columns_ref, proj_ref, *refs):
     outs, (ids, columns, proj, total, sems) = refs[:-5], refs[-5:]
     one, two = widths[0], widths[1]
     rest = widths[2] + widths[3]
@@ -99,6 +99,13 @@
         outs[0][...] = total[...]
 
 
+def total_kernel(*refs):
+    total = refs[0][...]
+    for ref in refs[1:-1]:
+        total = total + ref[...]
+    refs[-1][...] = total.astype(BF16)
+
+
 def unpack_kernel(ids_ref, pick_ref):
     ids = ids_ref[...]
     slot, row, _ = placement(ids)
@@ -240,6 +247,10 @@
 
 def in_hbm(value):
     return pltpu.with_memory_space_constraint(value, pltpu.HBM)
+
+
+def in_vmem(value):
+    return pltpu.with_memory_space_constraint(value, pltpu.VMEM)
 
 
 def limit(mebibytes):
@@ -282,10 +293,11 @@
     else:
         columns = tokens
     me_index = me.reshape(1).astype(jnp.int32)
+    mine_index = mine.reshape(1).astype(jnp.int32)
     parts = pl.pallas_call(
         functools.partial(partial_kernel, widths, spread),
         out_shape=shapes(*([((chunk, packed), F32)] * members if spread else [((CAP, packed), F32)])),
-        in_specs=[SMEM, HBM, HBM, HBM],
+        in_specs=[SMEM, SMEM, HBM, HBM, HBM],
         out_specs=[VMEM] * (members if spread else 1),
         scratch_shapes=[
             pltpu.VMEM((1, count), jnp.int32),
@@ -297,7 +309,7 @@
         compiler_params=limit(8),
         cost_estimate=cost(2 * count * features * 2 * packed, 4 * features * packed),
         name="partial",
-    )(me_index, in_hbm(ids), in_hbm(columns), in_hbm(tail_proj.T))
+    )(me_index, mine_index, in_hbm(ids), in_hbm(columns), in_hbm(tail_proj.T))
     if not spread:
         parts = [
             lax.dynamic_slice_in_dim(parts[0], (me ^ step) * chunk, chunk, 0) for step in range(members)
@@ -312,7 +324,6 @@
     steps = [step for step in range(0, groups, 2)]
     far = [exchange(head_weight, "batch", groups, step) for step in steps[1:]]
     near = exchange(head_weight, "batch", groups, 1)
-    mine_index = mine.reshape(1).astype(jnp.int32)
     vocab = head_weight.shape[1]
     depth = head_weight.shape[0]
     head_start = pl.pallas_call(
@@ -337,7 +348,15 @@
         cluster_weight, tokens, (((0,), (1,)), ((), ())), preferred_element_type=F32
     )
     arrived, head_start, cluster_logits = lax.optimization_barrier((arrived, head_start, cluster_logits))
-    own = sum(arrived[1:], arrived[0]).astype(BF16)
+    own = pl.pallas_call(
+        total_kernel,
+        out_shape=shapes(((chunk, packed), BF16))[0],
+        in_specs=[VMEM] * len(arrived),
+        out_specs=VMEM,
+        compiler_params=limit(2),
+        cost_estimate=cost(chunk * packed * len(arrived), 4 * chunk * packed * len(arrived)),
+        name="total",
+    )(*map(in_vmem, arrived))
     evens = [own] + [exchange(own, "vocab", members, step) for step in range(2, members, 2)]
     _, far = lax.optimization_barrier((evens[-1], far))
     chunks = []
@@ -357,7 +376,7 @@
         compiler_params=limit(6),
         cost_estimate=cost(2 * count * vocab * depth * len(far), depth * vocab * 4),
         name="head_more",
-    )(mine_index, tokens, *far, head_start)
+    )(mine_index, tokens, *map(in_vmem, far), head_start)
     head_logits, head_stats = pl.pallas_call(
         functools.partial(head_last_kernel, tuple(step ^ 1 for step in steps[1:])),
         out_shape=shapes(((count, vocab), F32), ((2 * SUBLANES, CAP), F32)),

time: 65.1 us -> 64.8 us (level)
  waiting for transfers between devices: 19.3 us -> 23.1 us
  Pallas kernels: 11.6 us -> 8.47 us
  other arithmetic: 1.12 us -> 0.19 us
    ppermute x20, waiting for transfers between devices: 19.3 us -> 23.1 us  [exchange(): return lax.ppermute(value, axis, [(at, at ^ step) for at in range(size)])]
    pallas_call x1, Pallas kernels: 2.56 us -> 0.85 us  [shards(): pl.pallas_call(functools.partial(head_first_kernel, (0, 1)), out_shape=sh...]
    pallas_call x1, Pallas kernels: 1.97 us -> 0.5 us  [shards(): pl.pallas_call(functools.partial(head_more_kernel, tuple(steps[1:])), out...]
    convert_element_type x1 -> x0, other arithmetic: 0.93 us -> none  [shards(): own = sum(arrived[1:], arrived[0]).astype(BF16)]
  transfers between devices with their start and end apart: 20 -> 20, of which waited for: 9 -> 10; matrix products, arithmetic and copies ran while one was open for 3% -> 1% of each run, Pallas kernels for 9% -> 4%
where the time goes in v1:
time: 64.8 us; the launch traced here: 64.6 us
  starting transfers between devices  31.2 us (48%)
  waiting for transfers between devices  23.1 us (36%)
  Pallas kernels  8.47 us (13%)
  between operations  0.84 us (1%)
  matrix products  0.77 us (1%)
    ppermute x20, starting transfers between devices, exchange(): return lax.ppermute(value, axis, [(at, at ^ step) for at in range(size)])  31.2 us
    ppermute x20, waiting for transfers between devices, exchange(): return lax.ppermute(value, axis, [(at, at ^ step) for at in range(size)])  23.1 us
    pallas_call x1, Pallas kernels, shards(): pl.pallas_call(functools.partial(partial_kernel, widths, spread), out_sha...  3.14 us
    pallas_call x1, Pallas kernels, shards(): pl.pallas_call(output_kernel, out_shape=shapes(*out_shapes), in_specs=[VM...  1.69 us
  transfers between devices with their start and end apart: 20, of which 10 were waited for; matrix products, arithmetic and copies ran while one was open for 1% of the time, Pallas kernels for 4%

profile of v1, /device:TPU:0, one launch (start us, length us, event | category | flops | bytes accessed | tf_op | source)
XLA Modules:
  0.0 64.6 jit_solution(4310123615247222382)
XLA Ops:
  0.7 3.1 %partial.1 = (f32[16,1920]{1,0:T(8,128)S(1)}, f32[16,1920]{1,0:T(8,128)S(1)}, f32[16,1920]{1,0:T(8,128)S(1)}, f32[16,1920]{1,0:T(8,128)S(1)}, f32[16,1920]{1,0:T...) custom-call(s32[1]{0:T(128)} %bitcast.1.me_ref, s32[1]{0:T(128)} %bitcast.mine_ref, ...), custom_call_target="tpu_custom_call" | custom-call | flops 1258291200 | bytes 4915200 | tf_op jit(solution)/shard_map/partial/pallas_call | solution.py:297
  3.8 0.6 collective-permute-start.7
  4.4 2.5 %collective-permute-start.9 = (bf16[1280,512]{1,0:T(8,128)(2,1)S(1)}, bf16[1280,512]{1,0:T(8,128)(2,1)S(1)}, u32[]{:S(2)}, u32[]{:S(2)}) collective-permute-start(bf16[1280,512]{1,0:T(8,128)(2,1)S(1)} %copy-done.4), channel_id=1, source_target_pairs={{0,2},{1,3},{2,0},{3,1},{4,6},{5,7},{6,4},{7,5},{8,10},{9,11},{10,... | collective-permute-start | bytes 3932168 | tf_op jit(solution)/shard_map/ppermute | solution.py:287
  6.9 1.5 %collective-permute-start.1 = (f32[16,1920]{1,0:T(8,128)S(1)}, f32[16,1920]{1,0:T(8,128)S(1)}, u32[]{:S(2)}, u32[]{:S(2)}) collective-permute-start(f32[16,1920]{1,0:T(8,128)S(1)} %get-tuple-element.47), channel_id=1, source_target_pairs={{0,4},{4,0},{8,12},{12,8},{16,20},{20,16},{24,28},{28,24},{1,5},{5... | collective-permute-start | bytes 368648 | tf_op jit(solution)/shard_map/ppermute | solution.py:287
  9.0 1.5 %collective-permute-start.5 = (f32[16,1920]{1,0:T(8,128)S(1)}, f32[16,1920]{1,0:T(8,128)S(1)}, u32[]{:S(2)}, u32[]{:S(2)}) collective-permute-start(f32[16,1920]{1,0:T(8,128)S(1)} %get-tuple-element.51), channel_id=1, source_target_pairs={{0,4},{4,0},{8,12},{12,8},{16,20},{20,16},{24,28},{28,24},{1,5},{5... | collective-permute-start | bytes 368648 | tf_op jit(solution)/shard_map/ppermute | solution.py:287
  10.5 2.6 %collective-permute-done.1 = f32[16,1920]{1,0:T(8,128)S(1)} collective-permute-done((f32[16,1920]{1,0:T(8,128)S(1)}, f32[16,1920]{1,0:T(8,128)S(1)}, u32[]{:S(2)}, u32[]{:S(2)}) %collective-permute-start.1) | collective-permute-done | bytes 122912 | tf_op jit(solution)/shard_map/ppermute | solution.py:287
  13.1 1.5 %collective-permute-start = (f32[16,1920]{1,0:T(8,128)S(1)}, f32[16,1920]{1,0:T(8,128)S(1)}, u32[]{:S(2)}, u32[]{:S(2)}) collective-permute-start(f32[16,1920]{1,0:T(8,128)S(1)} %get-tuple-element.45), channel_id=1, source_target_pairs={{0,4},{4,0},{8,12},{12,8},{16,20},{20,16},{24,28},{28,24},{1,5},{5... | collective-permute-start | bytes 368648 | tf_op jit(solution)/shard_map/ppermute | solution.py:287
  14.7 1.1 %collective-permute-done.3 = f32[16,1920]{1,0:T(8,128)S(1)} collective-permute-done((f32[16,1920]{1,0:T(8,128)S(1)}, f32[16,1920]{1,0:T(8,128)S(1)}, u32[]{:S(2)}, u32[]{:S(2)}) %collective-permute-start.3) | collective-permute-done | bytes 122912 | tf_op jit(solution)/shard_map/ppermute | solution.py:287
  15.8 3.6 %collective-permute-start.2 = (f32[16,1920]{1,0:T(8,128)S(1)}, f32[16,1920]{1,0:T(8,128)S(1)}, u32[]{:S(2)}, u32[]{:S(2)}) collective-permute-start(f32[16,1920]{1,0:T(8,128)S(1)} %add.19), channel_id=1, source_target_pairs={{0,24},{4,28},{8,16},{12,20},{16,8},{20,12},{24,0},{28,4},{1,25},{... | collective-permute-start | bytes 368648 | tf_op jit(solution)/shard_map/ppermute | solution.py:287
  19.4 1.6 %collective-permute-start.4 = (f32[16,1920]{1,0:T(8,128)S(1)}, f32[16,1920]{1,0:T(8,128)S(1)}, u32[]{:S(2)}, u32[]{:S(2)}) collective-permute-start(f32[16,1920]{1,0:T(8,128)S(1)} %add.20), channel_id=1, source_target_pairs={{0,16},{4,20},{8,24},{12,28},{16,0},{20,4},{24,8},{28,12},{1,17},{... | collective-permute-start | bytes 368648 | tf_op jit(solution)/shard_map/ppermute | solution.py:287
  21.0 1.6 %collective-permute-start.6 = (f32[16,1920]{1,0:T(8,128)S(1)}, f32[16,1920]{1,0:T(8,128)S(1)}, u32[]{:S(2)}, u32[]{:S(2)}) collective-permute-start(f32[16,1920]{1,0:T(8,128)S(1)} %add.21), channel_id=1, source_target_pairs={{0,8},{4,12},{8,0},{12,4},{16,24},{20,28},{24,16},{28,20},{1,9},{5... | collective-permute-start | bytes 368648 | tf_op jit(solution)/shard_map/ppermute | solution.py:287
  22.7 0.8 %fusion.2.cluster_ref = f32[4,256]{1,0:T(4,128)S(1)} fusion(bf16[5120,4]{0,1:T(4,128)(2,1)S(1)} %copy-done, bf16[256,5120]{1,0:T(8,128)(2,1)S(1)} %copy-done.1), kind=kOutput, calls=%fused_computation.11 | convolution fusion | flops 10485760 | bytes 2666496 | tf_op jit(solution)/shard_map/dot_general | solution.py:347
  23.5 0.8 %head_first.1.refs_1_ = f32[256,512]{1,0:T(8,128)S(1)} custom-call(s32[1]{0:T(128)} %bitcast.mine_ref, bf16[256,5120]{1,0:T(8,128)(2,1)S(1)} %copy-done.1, bf16[1280,512]{1,0:T(8,128)(2,1)S(1)} %copy-done.4, bf16[1280,512]{1,0:T(8,128)(2,1)S(1)} %collective-permute-done.7.refs_1_), custom_call_target="tpu_custom_call" | custom-call | flops 671088640 | bytes 2621440 | tf_op jit(solution)/shard_map/head_first/pallas_call | solution.py:329
  24.4 4.0 %collective-permute-done.4.refs_2_ = f32[16,1920]{1,0:T(8,128)S(1)} collective-permute-done((f32[16,1920]{1,0:T(8,128)S(1)}, f32[16,1920]{1,0:T(8,128)S(1)}, u32[]{:S(2)}, u32[]{:S(2)}) %collective-permute-start.4) | collective-permute-done | bytes 122912 | tf_op jit(solution)/shard_map/ppermute | solution.py:287
  28.5 3.5 %collective-permute-start.8 = (bf16[16,1920]{1,0:T(8,128)(2,1)S(1)}, bf16[16,1920]{1,0:T(8,128)(2,1)S(1)}, u32[]{:S(2)}, u32[]{:S(2)}) collective-permute-start(bf16[16,1920]{1,0:T(8,128)(2,1)S(1)} %total.1.refs_0_), channel_id=1, source_target_pairs={{0,24},{4,28},{8,16},{12,20},{16,8},{20,12},{24,0},{28,4},{1,25},{... | collective-permute-start | bytes 184328 | tf_op jit(solution)/shard_map/ppermute | solution.py:287
  32.0 4.3 %collective-permute-done.9.refs_0_ = bf16[1280,512]{1,0:T(8,128)(2,1)S(1)} collective-permute-done((bf16[1280,512]{1,0:T(8,128)(2,1)S(1)}, bf16[1280,512]{1,0:T(8,128)(2,1)S(1)}, u32[]{:S(2)}, u32[]{:S(2)}) %collective-permute-start.9) | collective-permute-done | bytes 1310752 | tf_op jit(solution)/shard_map/ppermute | solution.py:287
  36.3 1.8 %collective-permute-start.12 = (bf16[16,1920]{1,0:T(8,128)(2,1)S(1)}, bf16[16,1920]{1,0:T(8,128)(2,1)S(1)}, u32[]{:S(2)}, u32[]{:S(2)}) collective-permute-start(bf16[16,1920]{1,0:T(8,128)(2,1)S(1)} %total.1.refs_0_), channel_id=1, source_target_pairs={{0,8},{4,12},{8,0},{12,4},{16,24},{20,28},{24,16},{28,20},{1,9},{5... | collective-permute-start | bytes 184328 | tf_op jit(solution)/shard_map/ppermute | solution.py:287
  38.2 2.6 %collective-permute-start.14 = (bf16[16,1920]{1,0:T(8,128)(2,1)S(1)}, bf16[16,1920]{1,0:T(8,128)(2,1)S(1)}, u32[]{:S(2)}, u32[]{:S(2)}) collective-permute-start(bf16[16,1920]{1,0:T(8,128)(2,1)S(1)} %total.1.refs_0_), channel_id=1, source_target_pairs={{0,16},{4,20},{8,24},{12,28},{16,0},{20,4},{24,8},{28,12},{1,17},{... | collective-permute-start | bytes 184328 | tf_op jit(solution)/shard_map/ppermute | solution.py:287
  40.7 1.5 %collective-permute-start.11 = (bf16[16,1920]{1,0:T(8,128)(2,1)S(1)}, bf16[16,1920]{1,0:T(8,128)(2,1)S(1)}, u32[]{:S(2)}, u32[]{:S(2)}) collective-permute-start(bf16[16,1920]{1,0:T(8,128)(2,1)S(1)} %total.1.refs_0_), channel_id=1, source_target_pairs={{0,4},{4,0},{8,12},{12,8},{16,20},{20,16},{24,28},{28,24},{1,5},{5... | collective-permute-start | bytes 184328 | tf_op jit(solution)/shard_map/ppermute | solution.py:287
  42.8 1.5 %collective-permute-start.13 = (bf16[16,1920]{1,0:T(8,128)(2,1)S(1)}, bf16[16,1920]{1,0:T(8,128)(2,1)S(1)}, u32[]{:S(2)}, u32[]{:S(2)}) collective-permute-start(bf16[16,1920]{1,0:T(8,128)(2,1)S(1)} %collective-permute-done.12.refs_2_), channel_id=1, source_target_pairs={{0,4},{4,0},{8,12},{12,8},{16,20},{20,16},{24,28},{28,24},{1,5},{5... | collective-permute-start | bytes 184328 | tf_op jit(solution)/shard_map/ppermute | solution.py:287
  44.6 1.5 %collective-permute-start.15 = (bf16[16,1920]{1,0:T(8,128)(2,1)S(1)}, bf16[16,1920]{1,0:T(8,128)(2,1)S(1)}, u32[]{:S(2)}, u32[]{:S(2)}) collective-permute-start(bf16[16,1920]{1,0:T(8,128)(2,1)S(1)} %collective-permute-done.14.refs_4_), channel_id=1, source_target_pairs={{0,4},{4,0},{8,12},{12,8},{16,20},{20,16},{24,28},{28,24},{1,5},{5... | collective-permute-start | bytes 184328 | tf_op jit(solution)/shard_map/ppermute | solution.py:287
  47.1 1.2 %collective-permute-done.13.refs_3_ = bf16[16,1920]{1,0:T(8,128)(2,1)S(1)} collective-permute-done((bf16[16,1920]{1,0:T(8,128)(2,1)S(1)}, bf16[16,1920]{1,0:T(8,128)(2,1)S(1)}, u32[]{:S(2)}, u32[]{:S(2)}) %collective-permute-start.13) | collective-permute-done | bytes 61472 | tf_op jit(solution)/shard_map/ppermute | solution.py:287
  48.3 0.7 %collective-permute-done.15.refs_5_ = bf16[16,1920]{1,0:T(8,128)(2,1)S(1)} collective-permute-done((bf16[16,1920]{1,0:T(8,128)(2,1)S(1)}, bf16[16,1920]{1,0:T(8,128)(2,1)S(1)}, u32[]{:S(2)}, u32[]{:S(2)}) %collective-permute-start.15) | collective-permute-done | bytes 61472 | tf_op jit(solution)/shard_map/ppermute | solution.py:287
  48.9 1.1 %scores.1 = (f32[128,512]{1,0:T(8,128)S(1)}, f32[128,1024]{1,0:T(8,128)S(1)}, f32[128,1024]{1,0:T(8,128)S(1)}, f32[128,1024]{1,0:T(8,128)S(1)}, f32[16,128]{1,0:T(8,128)S(1)}) custom-call(s32[1]{0:T(128)} %bitcast.1.me_ref, bf16[256,256]{1,0:T(8,128)(2,1)S(1)} %unpack.1.pick_ref, bf16[1280,512]{1,0:T(8,128)(2,1)S(1)} %copy-done.2, ...), custom_call_target="tpu_custom_call" | custom-call | flops 461373440 | bytes 3604480 | tf_op jit(solution)/shard_map/scores/pallas_call | solution.py:390
  50.1 0.7 %head_last.1 = (f32[256,512]{1,0:T(8,128)S(1)}, f32[16,128]{1,0:T(8,128)S(1)}) custom-call(s32[1]{0:T(128)} %bitcast.mine_ref, bf16[256,5120]{1,0:T(8,128)(2,1)S(1)} %copy-done.1, bf16[1280,512]{1,0:T(8,128)(2,1)S(1)} %collective-permute-done.10.refs_0_, f32[256,512]{1,0:T(8,128)S(1)} %head_more.1.refs_1_), custom_call_target="tpu_custom_call" | custom-call | flops 335544320 | bytes 2621440 | tf_op jit(solution)/shard_map/head_last/pallas_call | solution.py:380
  50.9 1.4 %collective-permute-start.17 = (f32[16,128]{1,0:T(8,128)S(1)}, f32[16,128]{1,0:T(8,128)S(1)}, u32[]{:S(2)}, u32[]{:S(2)}) collective-permute-start(f32[16,128]{1,0:T(8,128)S(1)} %broadcast_select_fusion), channel_id=1, source_target_pairs={{0,4},{4,0},{8,12},{12,8},{16,20},{20,16},{24,28},{28,24},{1,5},{5... | collective-permute-start | bytes 24584 | tf_op jit(solution)/shard_map/ppermute | solution.py:287
  52.3 2.3 %collective-permute-done.17 = f32[16,128]{1,0:T(8,128)S(1)} collective-permute-done((f32[16,128]{1,0:T(8,128)S(1)}, f32[16,128]{1,0:T(8,128)S(1)}, u32[]{:S(2)}, u32[]{:S(2)}) %collective-permute-start.17) | collective-permute-done | bytes 8224 | tf_op jit(solution)/shard_map/ppermute | solution.py:287
  54.6 0.5 collective-permute-start.18
  55.1 3.2 %collective-permute-done.18 = f32[16,128]{1,0:T(8,128)S(1)} collective-permute-done((f32[16,128]{1,0:T(8,128)S(1)}, f32[16,128]{1,0:T(8,128)S(1)}, u32[]{:S(2)}, u32[]{:S(2)}) %collective-permute-start.18) | collective-permute-done | bytes 8224 | tf_op jit(solution)/shard_map/ppermute | solution.py:287
  58.3 1.3 %collective-permute-start.19 = (f32[16,128]{1,0:T(8,128)S(1)}, f32[16,128]{1,0:T(8,128)S(1)}, u32[]{:S(2)}, u32[]{:S(2)}) collective-permute-start(f32[16,128]{1,0:T(8,128)S(1)} %pad_maximum_fusion.1.own_ref), channel_id=1, source_target_pairs={{0,16},{4,20},{8,24},{12,28},{16,0},{20,4},{24,8},{28,12},{1,17},{... | collective-permute-start | bytes 24584 | tf_op jit(solution)/shard_map/ppermute | solution.py:287
  59.6 3.4 %collective-permute-done.19.other_ref = f32[16,128]{1,0:T(8,128)S(1)} collective-permute-done((f32[16,128]{1,0:T(8,128)S(1)}, f32[16,128]{1,0:T(8,128)S(1)}, u32[]{:S(2)}, u32[]{:S(2)}) %collective-permute-start.19) | collective-permute-done | bytes 8224 | tf_op jit(solution)/shard_map/ppermute | solution.py:287
  62.9 1.7 %outputs.1 = (f32[256,512]{1,0:T(8,128)}, f32[128,512]{1,0:T(8,128)}, f32[128,1024]{1,0:T(8,128)}, f32[128,1024]{1,0:T(8,128)}, f32[128,1024]{1,0:T(8,128)}) custom-call(f32[16,128]{1,0:T(8,128)S(1)} %pad_maximum_fusion.1.own_ref, f32[16,128]{1,0:T(8,128)S(1)} %collective-permute-done.19.other_ref, s32[1,256]{1,0:T(1,128)S(1)} %bitcast.8, ...), custom_call_target="tpu_custom_call" | custom-call | flops 1048576 | bytes 8388608 | tf_op jit(solution)/shard_map/outputs/pallas_call | solution.py:411
  (43 shorter events, 2.5 us)
Async XLA Ops:
  0.6 22.0 %copy-start = (bf16[5120,4]{0,1:T(4,128)(2,1)S(1)}, bf16[5120,4]{0,1:T(4,128)(2,1)}, u32[]{:S(2)}) copy-start(bf16[5120,4]{0,1:T(4,128)(2,1)} %param.12) | copy-start | bytes 122884
  0.7 3.2 %copy-start.4 = (bf16[1280,512]{1,0:T(8,128)(2,1)S(1)}, bf16[1280,512]{1,0:T(8,128)(2,1)}, u32[]{:S(2)}) copy-start(bf16[1280,512]{1,0:T(8,128)(2,1)} %refs_0_) | copy-start | bytes 3932164
  0.7 22.0 %copy-start.1 = (bf16[256,5120]{1,0:T(8,128)(2,1)S(1)}, bf16[256,5120]{1,0:T(8,128)(2,1)}, u32[]{:S(2)}) copy-start(bf16[256,5120]{1,0:T(8,128)(2,1)} %tokens_ref.5) | copy-start | bytes 7864324
  3.8 19.7 %collective-permute-start.7 = (bf16[1280,512]{1,0:T(8,128)(2,1)S(1)}, bf16[1280,512]{1,0:T(8,128)(2,1)S(1)}, u32[]{:S(2)}, u32[]{:S(2)}) collective-permute-start(bf16[1280,512]{1,0:T(8,128)(2,1)S(1)} %copy-done.4), channel_id=1, source_target_pairs={{0,1},{1,0},{2,3},{3,2},{4,5},{5,4},{6,7},{7,6},{8,9},{9,8},{10,11... | collective-permute-start | bytes 3932168 | tf_op jit(solution)/shard_map/ppermute | solution.py:287
  4.4 31.9 %collective-permute-start.9 = (bf16[1280,512]{1,0:T(8,128)(2,1)S(1)}, bf16[1280,512]{1,0:T(8,128)(2,1)S(1)}, u32[]{:S(2)}, u32[]{:S(2)}) collective-permute-start(bf16[1280,512]{1,0:T(8,128)(2,1)S(1)} %copy-done.4), channel_id=1, source_target_pairs={{0,2},{1,3},{2,0},{3,1},{4,6},{5,7},{6,4},{7,5},{8,10},{9,11},{10,... | collective-permute-start | bytes 3932168 | tf_op jit(solution)/shard_map/ppermute | solution.py:287
  6.9 6.2 %collective-permute-start.1 = (f32[16,1920]{1,0:T(8,128)S(1)}, f32[16,1920]{1,0:T(8,128)S(1)}, u32[]{:S(2)}, u32[]{:S(2)}) collective-permute-start(f32[16,1920]{1,0:T(8,128)S(1)} %get-tuple-element.47), channel_id=1, source_target_pairs={{0,4},{4,0},{8,12},{12,8},{16,20},{20,16},{24,28},{28,24},{1,5},{5... | collective-permute-start | bytes 368648 | tf_op jit(solution)/shard_map/ppermute | solution.py:287
  8.5 7.3 %collective-permute-start.3 = (f32[16,1920]{1,0:T(8,128)S(1)}, f32[16,1920]{1,0:T(8,128)S(1)}, u32[]{:S(2)}, u32[]{:S(2)}) collective-permute-start(f32[16,1920]{1,0:T(8,128)S(1)} %get-tuple-element.49), channel_id=1, source_target_pairs={{0,4},{4,0},{8,12},{12,8},{16,20},{20,16},{24,28},{28,24},{1,5},{5... | collective-permute-start | bytes 368648 | tf_op jit(solution)/shard_map/ppermute | solution.py:287
  9.0 10.4 %collective-permute-start.5 = (f32[16,1920]{1,0:T(8,128)S(1)}, f32[16,1920]{1,0:T(8,128)S(1)}, u32[]{:S(2)}, u32[]{:S(2)}) collective-permute-start(f32[16,1920]{1,0:T(8,128)S(1)} %get-tuple-element.51), channel_id=1, source_target_pairs={{0,4},{4,0},{8,12},{12,8},{16,20},{20,16},{24,28},{28,24},{1,5},{5... | collective-permute-start | bytes 368648 | tf_op jit(solution)/shard_map/ppermute | solution.py:287
  13.1 7.9 %collective-permute-start = (f32[16,1920]{1,0:T(8,128)S(1)}, f32[16,1920]{1,0:T(8,128)S(1)}, u32[]{:S(2)}, u32[]{:S(2)}) collective-permute-start(f32[16,1920]{1,0:T(8,128)S(1)} %get-tuple-element.45), channel_id=1, source_target_pairs={{0,4},{4,0},{8,12},{12,8},{16,20},{20,16},{24,28},{28,24},{1,5},{5... | collective-permute-start | bytes 368648 | tf_op jit(solution)/shard_map/ppermute | solution.py:287
  15.8 8.6 %collective-permute-start.2 = (f32[16,1920]{1,0:T(8,128)S(1)}, f32[16,1920]{1,0:T(8,128)S(1)}, u32[]{:S(2)}, u32[]{:S(2)}) collective-permute-start(f32[16,1920]{1,0:T(8,128)S(1)} %add.19), channel_id=1, source_target_pairs={{0,24},{4,28},{8,16},{12,20},{16,8},{20,12},{24,0},{28,4},{1,25},{... | collective-permute-start | bytes 368648 | tf_op jit(solution)/shard_map/ppermute | solution.py:287
  19.4 9.0 %collective-permute-start.4 = (f32[16,1920]{1,0:T(8,128)S(1)}, f32[16,1920]{1,0:T(8,128)S(1)}, u32[]{:S(2)}, u32[]{:S(2)}) collective-permute-start(f32[16,1920]{1,0:T(8,128)S(1)} %add.20), channel_id=1, source_target_pairs={{0,16},{4,20},{8,24},{12,28},{16,0},{20,4},{24,8},{28,12},{1,17},{... | collective-permute-start | bytes 368648 | tf_op jit(solution)/shard_map/ppermute | solution.py:287
  21.0 7.4 %collective-permute-start.6 = (f32[16,1920]{1,0:T(8,128)S(1)}, f32[16,1920]{1,0:T(8,128)S(1)}, u32[]{:S(2)}, u32[]{:S(2)}) collective-permute-start(f32[16,1920]{1,0:T(8,128)S(1)} %add.21), channel_id=1, source_target_pairs={{0,8},{4,12},{8,0},{12,4},{16,24},{20,28},{24,16},{28,20},{1,9},{5... | collective-permute-start | bytes 368648 | tf_op jit(solution)/shard_map/ppermute | solution.py:287
  23.5 22.6 %copy-start.7 = (s32[256,1]{0,1:T(1,128)S(1)}, s32[256,1]{0,1:T(1,128)}, u32[]{:S(2)}) copy-start(s32[256,1]{0,1:T(1,128)} %param.10) | copy-start | bytes 3076
  28.5 7.9 %collective-permute-start.8 = (bf16[16,1920]{1,0:T(8,128)(2,1)S(1)}, bf16[16,1920]{1,0:T(8,128)(2,1)S(1)}, u32[]{:S(2)}, u32[]{:S(2)}) collective-permute-start(bf16[16,1920]{1,0:T(8,128)(2,1)S(1)} %total.1.refs_0_), channel_id=1, source_target_pairs={{0,24},{4,28},{8,16},{12,20},{16,8},{20,12},{24,0},{28,4},{1,25},{... | collective-permute-start | bytes 184328 | tf_op jit(solution)/shard_map/ppermute | solution.py:287
  36.3 13.8 %collective-permute-start.10 = (bf16[1280,512]{1,0:T(8,128)(2,1)S(1)}, bf16[1280,512]{1,0:T(8,128)(2,1)S(1)}, u32[]{:S(2)}, u32[]{:S(2)}) collective-permute-start(bf16[1280,512]{1,0:T(8,128)(2,1)S(1)} %collective-permute-done.9.refs_0_), channel_id=1, source_target_pairs={{0,1},{1,0},{2,3},{3,2},{4,5},{5,4},{6,7},{7,6},{8,9},{9,8},{10,11... | collective-permute-start | bytes 3932168 | tf_op jit(solution)/shard_map/ppermute | solution.py:287
  36.3 6.5 %collective-permute-start.12 = (bf16[16,1920]{1,0:T(8,128)(2,1)S(1)}, bf16[16,1920]{1,0:T(8,128)(2,1)S(1)}, u32[]{:S(2)}, u32[]{:S(2)}) collective-permute-start(bf16[16,1920]{1,0:T(8,128)(2,1)S(1)} %total.1.refs_0_), channel_id=1, source_target_pairs={{0,8},{4,12},{8,0},{12,4},{16,24},{20,28},{24,16},{28,20},{1,9},{5... | collective-permute-start | bytes 184328 | tf_op jit(solution)/shard_map/ppermute | solution.py:287
  38.2 6.4 %collective-permute-start.14 = (bf16[16,1920]{1,0:T(8,128)(2,1)S(1)}, bf16[16,1920]{1,0:T(8,128)(2,1)S(1)}, u32[]{:S(2)}, u32[]{:S(2)}) collective-permute-start(bf16[16,1920]{1,0:T(8,128)(2,1)S(1)} %total.1.refs_0_), channel_id=1, source_target_pairs={{0,16},{4,20},{8,24},{12,28},{16,0},{20,4},{24,8},{28,12},{1,17},{... | collective-permute-start | bytes 184328 | tf_op jit(solution)/shard_map/ppermute | solution.py:287
  40.7 6.3 %collective-permute-start.11 = (bf16[16,1920]{1,0:T(8,128)(2,1)S(1)}, bf16[16,1920]{1,0:T(8,128)(2,1)S(1)}, u32[]{:S(2)}, u32[]{:S(2)}) collective-permute-start(bf16[16,1920]{1,0:T(8,128)(2,1)S(1)} %total.1.refs_0_), channel_id=1, source_target_pairs={{0,4},{4,0},{8,12},{12,8},{16,20},{20,16},{24,28},{28,24},{1,5},{5... | collective-permute-start | bytes 184328 | tf_op jit(solution)/shard_map/ppermute | solution.py:287
  42.3 6.7 %collective-permute-start.16 = (bf16[16,1920]{1,0:T(8,128)(2,1)S(1)}, bf16[16,1920]{1,0:T(8,128)(2,1)S(1)}, u32[]{:S(2)}, u32[]{:S(2)}) collective-permute-start(bf16[16,1920]{1,0:T(8,128)(2,1)S(1)} %collective-permute-done.8.refs_6_), channel_id=1, source_target_pairs={{0,4},{4,0},{8,12},{12,8},{16,20},{20,16},{24,28},{28,24},{1,5},{5... | collective-permute-start | bytes 184328 | tf_op jit(solution)/shard_map/ppermute | solution.py:287
  42.8 5.5 %collective-permute-start.13 = (bf16[16,1920]{1,0:T(8,128)(2,1)S(1)}, bf16[16,1920]{1,0:T(8,128)(2,1)S(1)}, u32[]{:S(2)}, u32[]{:S(2)}) collective-permute-start(bf16[16,1920]{1,0:T(8,128)(2,1)S(1)} %collective-permute-done.12.refs_2_), channel_id=1, source_target_pairs={{0,4},{4,0},{8,12},{12,8},{16,20},{20,16},{24,28},{28,24},{1,5},{5... | collective-permute-start | bytes 184328 | tf_op jit(solution)/shard_map/ppermute | solution.py:287
  44.6 4.4 %collective-permute-start.15 = (bf16[16,1920]{1,0:T(8,128)(2,1)S(1)}, bf16[16,1920]{1,0:T(8,128)(2,1)S(1)}, u32[]{:S(2)}, u32[]{:S(2)}) collective-permute-start(bf16[16,1920]{1,0:T(8,128)(2,1)S(1)} %collective-permute-done.14.refs_4_), channel_id=1, source_target_pairs={{0,4},{4,0},{8,12},{12,8},{16,20},{20,16},{24,28},{28,24},{1,5},{5... | collective-permute-start | bytes 184328 | tf_op jit(solution)/shard_map/ppermute | solution.py:287
  46.5 2.4 %copy-start.2 = (bf16[1280,512]{1,0:T(8,128)(2,1)S(1)}, bf16[1280,512]{1,0:T(8,128)(2,1)}, u32[]{:S(2)}) copy-start(bf16[1280,512]{1,0:T(8,128)(2,1)} %one_ref.1) | copy-start | bytes 3932164
  46.5 2.4 %copy-start.3 = (bf16[640,1024]{1,0:T(8,128)(2,1)S(1)}, bf16[640,1024]{1,0:T(8,128)(2,1)}, u32[]{:S(2)}) copy-start(bf16[640,1024]{1,0:T(8,128)(2,1)} %two_ref.1) | copy-start | bytes 3932164
  46.5 2.4 %copy-start.5 = (bf16[320,1024]{1,0:T(8,128)(2,1)S(1)}, bf16[320,1024]{1,0:T(8,128)(2,1)}, u32[]{:S(2)}) copy-start(bf16[320,1024]{1,0:T(8,128)(2,1)} %three_ref.1) | copy-start | bytes 1966084
  46.5 2.4 %copy-start.6 = (bf16[160,1024]{1,0:T(8,128)(2,1)S(1)}, bf16[160,1024]{1,0:T(8,128)(2,1)}, u32[]{:S(2)}) copy-start(bf16[160,1024]{1,0:T(8,128)(2,1)} %four_ref.1) | copy-start | bytes 983044
  50.9 3.7 %collective-permute-start.17 = (f32[16,128]{1,0:T(8,128)S(1)}, f32[16,128]{1,0:T(8,128)S(1)}, u32[]{:S(2)}, u32[]{:S(2)}) collective-permute-start(f32[16,128]{1,0:T(8,128)S(1)} %broadcast_select_fusion), channel_id=1, source_target_pairs={{0,4},{4,0},{8,12},{12,8},{16,20},{20,16},{24,28},{28,24},{1,5},{5... | collective-permute-start | bytes 24584 | tf_op jit(solution)/shard_map/ppermute | solution.py:287
  54.6 3.7 %collective-permute-start.18 = (f32[16,128]{1,0:T(8,128)S(1)}, f32[16,128]{1,0:T(8,128)S(1)}, u32[]{:S(2)}, u32[]{:S(2)}) collective-permute-start(f32[16,128]{1,0:T(8,128)S(1)} %pad_maximum_fusion), channel_id=1, source_target_pairs={{0,8},{4,12},{8,0},{12,4},{16,24},{20,28},{24,16},{28,20},{1,9},{5... | collective-permute-start | bytes 24584 | tf_op jit(solution)/shard_map/ppermute | solution.py:287
  58.3 4.6 %collective-permute-start.19 = (f32[16,128]{1,0:T(8,128)S(1)}, f32[16,128]{1,0:T(8,128)S(1)}, u32[]{:S(2)}, u32[]{:S(2)}) collective-permute-start(f32[16,128]{1,0:T(8,128)S(1)} %pad_maximum_fusion.1.own_ref), channel_id=1, source_target_pairs={{0,16},{4,20},{8,24},{12,28},{16,0},{20,4},{24,8},{28,12},{1,17},{... | collective-permute-start | bytes 24584 | tf_op jit(solution)/shard_map/ppermute | solution.py:287

commit v2 on v1

--- a/solution.py
+++ b/solution.py
@@ -52,8 +52,8 @@
     return lax.dot_general(left, right, (((1,), (1,)), ((), ())), preferred_element_type=F32)
 
 
-def partial_kernel(widths, spread, me_ref, mine_ref, ids_ref, columns_ref, proj_ref, *refs):
-    outs, (ids, columns, proj, total, sems) = refs[:-5], refs[-5:]
+def partial_kernel(widths, spread, me_ref, mine_ref, ids_ref, columns_ref, proj_ref, head_ref, *refs):
+    outs, cuts, (ids, columns, proj, total, sems) = refs[:-7], refs[-7:-5], refs[-5:]
     one, two = widths[0], widths[1]
     rest = widths[2] + widths[3]
     features = columns.shape[1]
@@ -71,6 +71,10 @@
                 proj_ref.at[pl.ds(begin, size), :], proj.at[pl.ds(begin, size), :], sems.at[1 + at]
             )
         )
+    begin = 0
+    for at, cut in enumerate(cuts):
+        copies.append(pltpu.make_async_copy(head_ref.at[pl.ds(begin, cut.shape[0]), :], cut, sems.at[5 + at]))
+        begin += cut.shape[0]
     for copy in copies:
         copy.start()
     first_copy.wait()
@@ -92,28 +96,30 @@
     total[:, one : one + rest] = jnp.where(number < counts[1:2], whole[:, :rest], others[CAP:])
     if spread:
         chunk = outs[0].shape[0]
-        for step, out in enumerate(outs):
-            begin = pl.multiple_of((me_ref[0] ^ step) * chunk, chunk)
-            out[...] = total[pl.ds(begin, chunk), :]
+        step = 0
+        for out in outs:
+            for first in range(0, out.shape[0], chunk):
+                begin = pl.multiple_of((me_ref[0] ^ step) * chunk, chunk)
+                out[first : first + chunk, :] = total[pl.ds(begin, chunk), :]
+                step += 1
     else:
         outs[0][...] = total[...]
+    for copy in copies[4:]:
+        copy.wait()
 
 
 def total_kernel(*refs):
-    total = refs[0][...]
+    total = refs[0][: refs[-1].shape[0]]
     for ref in refs[1:-1]:
         total = total + ref[...]
     refs[-1][...] = total.astype(BF16)
 
 
-def unpack_kernel(ids_ref, pick_ref):
+def unpack_kernel(cluster, ids_ref, pick_ref):
     ids = ids_ref[...]
     slot, row, _ = placement(ids)
-    matrix = row_matrix(row)
-    where = iota((CAP, ids.shape[1]), 0)
-    for at, cluster in enumerate((2, 3)):
-        own = ((ids == cluster) & (slot == where)).astype(BF16)
-        pick_ref[at * CAP : (at + 1) * CAP, :] = contract_last(own, matrix).astype(BF16)
+    own = ((ids == cluster) & (slot == iota((CAP, ids.shape[1]), 0))).astype(BF16)
+    pick_ref[...] = contract_last(own, row_matrix(row)).astype(BF16)
 
 
 def pack_columns(columns):
@@ -129,18 +135,32 @@
     return top, jnp.sum(jnp.exp(values - top), axis=1, keepdims=True)
 
 
-def head_more_kernel(steps, mine_ref, tokens_ref, *refs):
+def add_pieces(total, places, mine_ref, tokens_ref, weights):
+    for (step, depth, first), weight in zip(places, weights):
+        begin = pl.multiple_of((mine_ref[0] ^ step) * depth + first, LANES)
+        total = total + matmul(tokens_ref[:, pl.ds(begin, weight.shape[0])], weight[...])
+    return total
+
+
+def head_more_kernel(places, mine_ref, tokens_ref, *refs):
     weights, start, out = refs[:-2], refs[-2], refs[-1]
-    total = start[...]
-    for step, weight in zip(steps, weights):
-        depth = weight.shape[0]
-        begin = pl.multiple_of((mine_ref[0] ^ step) * depth, depth)
-        total = total + matmul(tokens_ref[:, pl.ds(begin, depth)], weight[...])
-    out[...] = total
+    out[...] = add_pieces(start[...], places, mine_ref, tokens_ref, weights)
 
 
 def head_first_kernel(steps, mine_ref, tokens_ref, *refs):
-    weights, out = refs[:-1], refs[-1]
+    count = len(steps)
+    weights, sources, out, kept, sems = (
+        refs[:count],
+        refs[count : count + CLUSTERS],
+        refs[count + CLUSTERS],
+        refs[count + CLUSTERS + 1 : -1],
+        refs[-1],
+    )
+    copies = [
+        pltpu.make_async_copy(source, value, sems.at[at]) for at, (source, value) in enumerate(zip(sources, kept))
+    ]
+    for copy in copies:
+        copy.start()
     total = None
     for step, weight in zip(steps, weights):
         depth = weight.shape[0]
@@ -148,22 +168,20 @@
         part = matmul(tokens_ref[:, pl.ds(begin, depth)], weight[...])
         total = part if total is None else total + part
     out[...] = total
-
-
-def head_last_kernel(steps, mine_ref, tokens_ref, *refs):
+    for copy in copies:
+        copy.wait()
+
+
+def head_last_kernel(places, mine_ref, tokens_ref, *refs):
     weights, start, out, stats = refs[:-3], refs[-3], refs[-2], refs[-1]
-    total = start[...]
-    for step, weight in zip(steps, weights):
-        depth = weight.shape[0]
-        begin = pl.multiple_of((mine_ref[0] ^ step) * depth, depth)
-        total = total + matmul(tokens_ref[:, pl.ds(begin, depth)], weight[...])
+    total = add_pieces(start[...], places, mine_ref, tokens_ref, weights)
     out[...] = total
     top, mass = row_stats(total)
     stats[:SUBLANES] = pack_columns((top[:CAP], top[CAP:]))
     stats[SUBLANES:] = pack_columns((mass[:CAP], mass[CAP:]))
 
 
-def score_kernel(widths, spread, me_ref, pick_ref, one_ref, two_ref, three_ref, four_ref, *refs):
+def score_kernel(widths, spread, me_ref, three_pick_ref, four_pick_ref, one_ref, two_ref, three_ref, four_ref, *refs):
     chunks = refs[:-6]
     scores, stats, joined = refs[-6:-2], refs[-2], refs[-1]
     if spread:
@@ -176,12 +194,11 @@
     one, two = widths[0], widths[1]
     rest = widths[2] + widths[3]
     small = jnp.concatenate([joined[:, :rest], joined[:, one : one + rest]], axis=0)
-    picked = matmul(pick_ref[...], small).astype(BF16)
     lefts = (
         joined[:, :one],
         joined[:, one : one + two],
-        picked[:CAP, : widths[2]],
-        picked[CAP:, widths[2] : rest],
+        matmul(three_pick_ref[...], small[:, : widths[2]]).astype(BF16),
+        matmul(four_pick_ref[...], small[:, widths[2] :]).astype(BF16),
     )
     tops, masses = [], []
     for left, weight, score in zip(lefts, (one_ref, two_ref, three_ref, four_ref), scores):
@@ -208,7 +225,12 @@
 
 
 def output_kernel(own_ref, other_ref, ids_ref, cluster_ref, head_ref, *refs):
-    scores, head_out, outs = refs[:CLUSTERS], refs[CLUSTERS], refs[CLUSTERS + 1 :]
+    scores, targets, values, sems = refs[:CLUSTERS], refs[CLUSTERS:9], refs[9:14], refs[14]
+    copies = [
+        pltpu.make_async_copy(value, target, sems.at[at])
+        for at, (value, target) in enumerate(zip(values, targets))
+    ]
+    head_out, outs = values[0], values[1:]
     ids = ids_ref[...]
     slot, _, counts = placement(ids)
     cluster_logits = cluster_ref[...]
@@ -230,6 +252,7 @@
     columns = columns_of(logs)
     head_out[:CAP] = head_ref[:CAP] - columns[:, 0:1]
     head_out[CAP:] = head_ref[CAP:] - columns[:, 1:2]
+    copies[0].start()
     own_logp = own_logit - log_total
     here = slot == iota((CAP, ids.shape[1]), 0)
     number = iota((CAP, 1), 0).astype(F32)
@@ -239,6 +262,9 @@
         outs[cluster][...] = jnp.where(
             number < counts[cluster : cluster + 1], scores[cluster][...] - shift, 0.0
         )
+        copies[1 + cluster].start()
+    for copy in copies:
+        copy.wait()
 
 
 def shapes(*pairs):
@@ -292,58 +318,67 @@
         columns = lax.dynamic_slice_in_dim(tokens, me * features, features, 1)
     else:
         columns = tokens
+    heights = [chunk, chunk, 2 * chunk] + [chunk] * (members - 4) if spread else [CAP]
     me_index = me.reshape(1).astype(jnp.int32)
     mine_index = mine.reshape(1).astype(jnp.int32)
-    parts = pl.pallas_call(
+    depth, vocab = head_weight.shape
+    large = depth * 3 // 4 // LANES * LANES
+    *parts, cut_one, cut_two = pl.pallas_call(
         functools.partial(partial_kernel, widths, spread),
-        out_shape=shapes(*([((chunk, packed), F32)] * members if spread else [((CAP, packed), F32)])),
-        in_specs=[SMEM, SMEM, HBM, HBM, HBM],
-        out_specs=[VMEM] * (members if spread else 1),
+        out_shape=[pltpu.VMEM((rows, packed), F32) for rows in heights]
+        + [pltpu.VMEM((rows, vocab), BF16) for rows in (large, depth - large)],
+        in_specs=[SMEM, SMEM, HBM, HBM, HBM, HBM],
+        out_specs=[VMEM] * (len(heights) + 2),
         scratch_shapes=[
             pltpu.VMEM((1, count), jnp.int32),
             pltpu.VMEM((count, features), BF16),
             pltpu.VMEM(tail_proj.shape[::-1], BF16),
             pltpu.VMEM((CAP, packed), F32),
-            pltpu.SemaphoreType.DMA((5,)),
+            pltpu.SemaphoreType.DMA((7,)),
         ],
         compiler_params=limit(8),
         cost_estimate=cost(2 * count * features * 2 * packed, 4 * features * packed),
         name="partial",
-    )(me_index, mine_index, in_hbm(ids), in_hbm(columns), in_hbm(tail_proj.T))
+    )(me_index, mine_index, in_hbm(ids), in_hbm(columns), in_hbm(tail_proj.T), in_hbm(head_weight))
     if not spread:
-        parts = [
+        blocks = [
             lax.dynamic_slice_in_dim(parts[0], (me ^ step) * chunk, chunk, 0) for step in range(members)
         ]
+        parts = blocks[:2] + [jnp.concatenate(blocks[2:4], axis=0)] + blocks[4:]
     parts, head_weight = lax.optimization_barrier((parts, head_weight))
-    pairs = [
-        parts[step] + exchange(parts[step + 1], "vocab", members, 1)
-        for step in reversed(range(0, members, 2))
-    ][::-1]
-    arrived = [pairs[0]] + [exchange(pairs[at], "vocab", members, 2 * at) for at in reversed(range(1, members // 2))]
+    cuts = (cut_one, cut_two)
+    beside = exchange(parts[2], "vocab", members, 2)
+    last = exchange(parts[1] + beside[chunk:], "vocab", members, 1)
+    arrived = [beside, parts[0], last]
+    for step in range(members - 2, 2, -2):
+        pair = parts[step - 1] + exchange(parts[step], "vocab", members, 1)
+        arrived.append(exchange(pair, "vocab", members, step))
 
     steps = [step for step in range(0, groups, 2)]
-    far = [exchange(head_weight, "batch", groups, step) for step in steps[1:]]
+    far = [[exchange(cut, "batch", groups, step) for step in steps[1:]] for cut in cuts]
     near = exchange(head_weight, "batch", groups, 1)
-    vocab = head_weight.shape[1]
-    depth = head_weight.shape[0]
-    head_start = pl.pallas_call(
+    head_start, *out_weights = pl.pallas_call(
         functools.partial(head_first_kernel, (0, 1)),
-        out_shape=shapes(((count, vocab), F32))[0],
-        in_specs=[SMEM, VMEM, VMEM, VMEM],
-        out_specs=VMEM,
+        out_shape=[pltpu.VMEM((count, vocab), F32)]
+        + [pltpu.VMEM(weight.shape, weight.dtype) for weight in out_weights],
+        in_specs=[SMEM, VMEM, VMEM, VMEM] + [HBM] * CLUSTERS,
+        out_specs=[VMEM] * (1 + CLUSTERS),
+        scratch_shapes=[pltpu.SemaphoreType.DMA((CLUSTERS,))],
         compiler_params=limit(6),
         cost_estimate=cost(2 * count * vocab * depth * 2, depth * vocab * 4),
         name="head_first",
-    )(mine_index, tokens, head_weight, near)
-    pick = pl.pallas_call(
-        unpack_kernel,
-        out_shape=shapes(((2 * CAP, count), BF16))[0],
-        in_specs=[VMEM],
-        out_specs=VMEM,
-        compiler_params=limit(2),
-        cost_estimate=cost(2 * count * count * count * 2, 4 * count * count),
-        name="unpack",
-    )(ids)
+    )(mine_index, tokens, head_weight, near, *map(in_hbm, out_weights))
+    picks = [
+        pl.pallas_call(
+            functools.partial(unpack_kernel, cluster),
+            out_shape=pltpu.VMEM((CAP, count), BF16),
+            in_specs=[VMEM],
+            out_specs=VMEM,
+            compiler_params=limit(2),
+            cost_estimate=cost(2 * count * count * count, 4 * count * count),
+        )(ids)
+        for cluster in (2, 3)
+    ]
     cluster_logits = lax.dot_general(
         cluster_weight, tokens, (((0,), (1,)), ((), ())), preferred_element_type=F32
     )
@@ -358,7 +393,8 @@
         name="total",
     )(*map(in_vmem, arrived))
     evens = [own] + [exchange(own, "vocab", members, step) for step in range(2, members, 2)]
-    _, far = lax.optimization_barrier((evens[-1], far))
+    _, far[1] = lax.optimization_barrier((evens[-1], far[1]))
+    _, far[0] = lax.optimization_barrier((own, far[0]))
     chunks = []
     for value in evens:
         chunks += [value, exchange(value, "vocab", members, 1)]
@@ -367,30 +403,35 @@
         order = me ^ jnp.arange(members)
         chunks = [jnp.take(stacked, order, axis=0).reshape(CAP, packed)]
 
-    rest = [exchange(value, "batch", groups, 1) for value in far]
+    rest = [[exchange(value, "batch", groups, 1) for value in values] for values in far]
+    early = far[0] + rest[0] + far[1]
+    places = [
+        [(step ^ near, depth, first) for step in steps[1:]]
+        for first, near in ((0, 0), (0, 1), (large, 0), (large, 1))
+    ]
     head_more = pl.pallas_call(
-        functools.partial(head_more_kernel, tuple(steps[1:])),
+        functools.partial(head_more_kernel, sum(places[:3], [])),
         out_shape=shapes(((count, vocab), F32))[0],
-        in_specs=[SMEM] + [VMEM] * (len(far) + 2),
+        in_specs=[SMEM] + [VMEM] * (len(early) + 2),
         out_specs=VMEM,
         compiler_params=limit(6),
-        cost_estimate=cost(2 * count * vocab * depth * len(far), depth * vocab * 4),
+        cost_estimate=cost(2 * count * vocab * depth * 2, depth * vocab * 4),
         name="head_more",
-    )(mine_index, tokens, *map(in_vmem, far), head_start)
+    )(mine_index, tokens, *map(in_vmem, early), head_start)
     head_logits, head_stats = pl.pallas_call(
-        functools.partial(head_last_kernel, tuple(step ^ 1 for step in steps[1:])),
+        functools.partial(head_last_kernel, places[3]),
         out_shape=shapes(((count, vocab), F32), ((2 * SUBLANES, CAP), F32)),
-        in_specs=[SMEM] + [VMEM] * (len(rest) + 2),
+        in_specs=[SMEM] + [VMEM] * (len(rest[1]) + 2),
         out_specs=[VMEM] * 2,
         compiler_params=limit(6),
-        cost_estimate=cost(2 * count * vocab * depth * len(rest), depth * vocab * 4),
+        cost_estimate=cost(2 * count * vocab * depth * len(rest[1]), depth * vocab * 4),
         name="head_last",
-    )(mine_index, tokens, *rest, head_more)
+    )(mine_index, tokens, *rest[1], head_more)
     score_shapes = [((CAP, weight.shape[1]), F32) for weight in out_weights]
     *scores, stats = pl.pallas_call(
         functools.partial(score_kernel, widths, spread),
         out_shape=shapes(*score_shapes, ((2 * SUBLANES, CAP), F32)),
-        in_specs=[SMEM] + [VMEM] * (5 + len(chunks)),
+        in_specs=[SMEM] + [VMEM] * (6 + len(chunks)),
         out_specs=[VMEM] * (CLUSTERS + 1),
         scratch_shapes=[pltpu.VMEM((CAP, packed), BF16)],
         compiler_params=limit(6),
@@ -398,21 +439,23 @@
             2 * CAP * sum(weight.size for weight in out_weights), 2 * sum(weight.size for weight in out_weights)
         ),
         name="scores",
-    )(me_index, pick, *out_weights, *chunks)
+    )(me_index, *picks, *out_weights, *chunks)
 
     stats = jnp.where(lax.rem(iota(stats.shape, 0), SUBLANES) < 2, head_stats, stats)
-    step = 1
-    while 2 * step < members:
+    step = members // 2
+    while step > 1:
         stats = jnp.concatenate(merge(stats, exchange(stats, "vocab", members, step)), axis=0)
-        step = 2 * step
-    other = exchange(stats, "vocab", members, step)
+        step = step // 2
+    other = exchange(stats, "vocab", members, 1)
     out_shapes = [((count, vocab), F32)] + score_shapes
     return tuple(
         pl.pallas_call(
             output_kernel,
             out_shape=shapes(*out_shapes),
             in_specs=[VMEM] * (5 + CLUSTERS),
-            out_specs=[VMEM] * (1 + CLUSTERS),
+            out_specs=[HBM] * (1 + CLUSTERS),
+            scratch_shapes=[pltpu.VMEM(shape, kind) for shape, kind in out_shapes]
+            + [pltpu.SemaphoreType.DMA((1 + CLUSTERS,))],
             compiler_params=limit(6),
         cost_estimate=cost(count * vocab * 8, 8 * count * vocab * 8),
             name="outputs",

time: 64.8 us -> 70.8 us (1.093)
  waiting for transfers between devices: 23.1 us -> 29.5 us
  starting transfers between devices: 31.2 us -> 29.1 us
  Pallas kernels: 8.47 us -> 10.4 us
    ppermute x20 -> x21, waiting for transfers between devices: 23.1 us -> 29.5 us  [exchange(): return lax.ppermute(value, axis, [(at, at ^ step) for at in range(size)])]
    ppermute x20 -> x21, starting transfers between devices: 31.2 us -> 29.1 us  [exchange(): return lax.ppermute(value, axis, [(at, at ^ step) for at in range(size)])]
    pallas_call x4 -> x5, Pallas kernels: 2.47 us -> 4.24 us  [the longest x1 2.1 us: shards(): pl.pallas_call(functools.partial(head_first_kernel, (0, 1)), out_shape=[p...]
  transfers between devices with their start and end apart: 20 -> 21, of which waited for: 10 -> 10; matrix products, arithmetic and copies ran while one was open for 1% -> 1% of each run, Pallas kernels for 4% -> 7%
where the time goes in v2:
time: 70.8 us; the launch traced here: 70.7 us
  waiting for transfers between devices  29.5 us (42%)
  starting transfers between devices  29.1 us (41%)
  Pallas kernels  10.4 us (15%)
  matrix products  0.77 us (1%)
  between operations  0.76 us (1%)
    ppermute x21, waiting for transfers between devices, exchange(): return lax.ppermute(value, axis, [(at, at ^ step) for at in range(size)])  29.5 us
    ppermute x21, starting transfers between devices, exchange(): return lax.ppermute(value, axis, [(at, at ^ step) for at in range(size)])  29.1 us
    pallas_call x1, Pallas kernels, shards(): pl.pallas_call(functools.partial(partial_kernel, widths, spread), out_sha...  3.17 us
    pallas_call x1, Pallas kernels, shards(): pl.pallas_call(functools.partial(head_first_kernel, (0, 1)), out_shape=[p...  2.1 us
    pallas_call x1, Pallas kernels, shards(): pl.pallas_call(output_kernel, out_shape=shapes(*out_shapes), in_specs=[VM...  1.74 us
  transfers between devices with their start and end apart: 21, of which 10 were waited for; matrix products, arithmetic and copies ran while one was open for 1% of the time, Pallas kernels for 7%

profile of v2, /device:TPU:0, one launch (start us, length us, event | category | flops | bytes accessed | tf_op | source)
XLA Modules:
  0.0 70.7 jit_solution(186689177531264747)
XLA Ops:
  0.7 3.2 %partial.1 = (f32[16,1920]{1,0:T(8,128)S(1)}, f32[16,1920]{1,0:T(8,128)S(1)}, f32[32,1920]{1,0:T(8,128)S(1)}, f32[16,1920]{1,0:T(8,128)S(1)}, f32[16,1920]{1,0:T...) custom-call(s32[1]{0:T(128)} %bitcast.1.me_ref, ...), custom_call_target="tpu_custom_call" | custom-call | flops 1258291200 | bytes 4915200 | tf_op jit(solution)/shard_map/partial/pallas_call | solution.py:326
  3.9 0.6 collective-permute-start.6
  4.4 2.6 %collective-permute-start = (f32[32,1920]{1,0:T(8,128)S(1)}, f32[32,1920]{1,0:T(8,128)S(1)}, u32[]{:S(2)}, u32[]{:S(2)}) collective-permute-start(f32[32,1920]{1,0:T(8,128)S(1)} %get-tuple-element.50), channel_id=1, source_target_pairs={{0,8},{4,12},{8,0},{12,4},{16,24},{20,28},{24,16},{28,20},{1,9},{5... | collective-permute-start | bytes 737288 | tf_op jit(solution)/shard_map/ppermute | solution.py:313
  7.1 1.5 %collective-permute-start.2 = (f32[16,1920]{1,0:T(8,128)S(1)}, f32[16,1920]{1,0:T(8,128)S(1)}, u32[]{:S(2)}, u32[]{:S(2)}) collective-permute-start(f32[16,1920]{1,0:T(8,128)S(1)} %get-tuple-element.54), channel_id=1, source_target_pairs={{0,4},{4,0},{8,12},{12,8},{16,20},{20,16},{24,28},{28,24},{1,5},{5... | collective-permute-start | bytes 368648 | tf_op jit(solution)/shard_map/ppermute | solution.py:313
  9.1 1.5 %collective-permute-start.10 = (bf16[896,512]{1,0:T(8,128)(2,1)S(1)}, bf16[896,512]{1,0:T(8,128)(2,1)S(1)}, u32[]{:S(2)}, u32[]{:S(2)}) collective-permute-start(bf16[896,512]{1,0:T(8,128)(2,1)S(1)} %get-tuple-element.66), channel_id=1, source_target_pairs={{0,2},{1,3},{2,0},{3,1},{4,6},{5,7},{6,4},{7,5},{8,10},{9,11},{10,... | collective-permute-start | bytes 2752520 | tf_op jit(solution)/shard_map/ppermute | solution.py:313
  10.6 2.7 %collective-permute-done.2 = f32[16,1920]{1,0:T(8,128)S(1)} collective-permute-done((f32[16,1920]{1,0:T(8,128)S(1)}, f32[16,1920]{1,0:T(8,128)S(1)}, u32[]{:S(2)}, u32[]{:S(2)}) %collective-permute-start.2) | collective-permute-done | bytes 122912 | tf_op jit(solution)/shard_map/ppermute | solution.py:313
  13.3 2.5 %collective-permute-start.3 = (f32[16,1920]{1,0:T(8,128)S(1)}, f32[16,1920]{1,0:T(8,128)S(1)}, u32[]{:S(2)}, u32[]{:S(2)}) collective-permute-start(f32[16,1920]{1,0:T(8,128)S(1)} %add.16), channel_id=1, source_target_pairs={{0,24},{4,28},{8,16},{12,20},{16,8},{20,12},{24,0},{28,4},{1,25},{... | collective-permute-start | bytes 368648 | tf_op jit(solution)/shard_map/ppermute | solution.py:313
  15.8 1.9 %collective-permute-start.5 = (f32[16,1920]{1,0:T(8,128)S(1)}, f32[16,1920]{1,0:T(8,128)S(1)}, u32[]{:S(2)}, u32[]{:S(2)}) collective-permute-start(f32[16,1920]{1,0:T(8,128)S(1)} %add.17), channel_id=1, source_target_pairs={{0,16},{4,20},{8,24},{12,28},{16,0},{20,4},{24,8},{28,12},{1,17},{... | collective-permute-start | bytes 368648 | tf_op jit(solution)/shard_map/ppermute | solution.py:313
  17.8 1.6 %collective-permute-start.1 = (f32[16,1920]{1,0:T(8,128)S(1)}, f32[16,1920]{1,0:T(8,128)S(1)}, u32[]{:S(2)}, u32[]{:S(2)}) collective-permute-start(f32[16,1920]{1,0:T(8,128)S(1)} %slice_add_fusion), channel_id=1, source_target_pairs={{0,4},{4,0},{8,12},{12,8},{16,20},{20,16},{24,28},{28,24},{1,5},{5... | collective-permute-start | bytes 368648 | tf_op jit(solution)/shard_map/ppermute | solution.py:313
  19.4 0.8 %fusion.2.cluster_ref = f32[4,256]{1,0:T(4,128)S(1)} fusion(bf16[5120,4]{0,1:T(4,128)(2,1)S(1)} %copy-done, bf16[256,5120]{1,0:T(8,128)(2,1)S(1)} %copy-done.1), kind=kOutput, calls=%fused_computation.12 | convolution fusion | flops 10485760 | bytes 2666496 | tf_op jit(solution)/shard_map/dot_general | solution.py:382
  20.1 2.1 %head_first.1 = (f32[256,512]{1,0:T(8,128)S(1)}, bf16[1280,512]{1,0:T(8,128)(2,1)S(1)}, bf16[640,1024]{1,0:T(8,128)(2,1)S(1)}, bf16[320,1024]{1,0:T(8,128)(2,1)S(1)}, bf16[160,1024]{1,0:T(8,128)(2,1)S(1)}) custom-call(s32[1]{0:T(128)} %bitcast.mine_ref, bf16[256,5120]{1,0:T(8,128)(2,1)S(1)} %copy-done.1, bf16[1280,512]{1,0:T(8,128)(2,1)S(1)} %copy-done.2, ...), custom_call_target="tpu_custom_call" | custom-call | flops 671088640 | bytes 2621440 | tf_op jit(solution)/shard_map/head_first/pallas_call | solution.py:360
  22.3 3.5 %collective-permute-done.5.refs_4_ = f32[16,1920]{1,0:T(8,128)S(1)} collective-permute-done((f32[16,1920]{1,0:T(8,128)S(1)}, f32[16,1920]{1,0:T(8,128)S(1)}, u32[]{:S(2)}, u32[]{:S(2)}) %collective-permute-start.5) | collective-permute-done | bytes 122912 | tf_op jit(solution)/shard_map/ppermute | solution.py:313
  25.8 5.1 %collective-permute-done.10.refs_0_ = bf16[896,512]{1,0:T(8,128)(2,1)S(1)} collective-permute-done((bf16[896,512]{1,0:T(8,128)(2,1)S(1)}, bf16[896,512]{1,0:T(8,128)(2,1)S(1)}, u32[]{:S(2)}, u32[]{:S(2)}) %collective-permute-start.10) | collective-permute-done | bytes 917536 | tf_op jit(solution)/shard_map/ppermute | solution.py:313
  30.9 1.5 %collective-permute-start.8 = (bf16[384,512]{1,0:T(8,128)(2,1)S(1)}, bf16[384,512]{1,0:T(8,128)(2,1)S(1)}, u32[]{:S(2)}, u32[]{:S(2)}) collective-permute-start(bf16[384,512]{1,0:T(8,128)(2,1)S(1)} %get-tuple-element.64), channel_id=1, source_target_pairs={{0,2},{1,3},{2,0},{3,1},{4,6},{5,7},{6,4},{7,5},{8,10},{9,11},{10,... | collective-permute-start | bytes 1179656 | tf_op jit(solution)/shard_map/ppermute | solution.py:313
  32.4 2.5 %collective-permute-start.7 = (bf16[16,1920]{1,0:T(8,128)(2,1)S(1)}, bf16[16,1920]{1,0:T(8,128)(2,1)S(1)}, u32[]{:S(2)}, u32[]{:S(2)}) collective-permute-start(bf16[16,1920]{1,0:T(8,128)(2,1)S(1)} %total.1.refs_0_), channel_id=1, source_target_pairs={{0,24},{4,28},{8,16},{12,20},{16,8},{20,12},{24,0},{28,4},{1,25},{... | collective-permute-start | bytes 184328 | tf_op jit(solution)/shard_map/ppermute | solution.py:313
  34.9 7.6 %collective-permute-done.8.refs_2_ = bf16[384,512]{1,0:T(8,128)(2,1)S(1)} collective-permute-done((bf16[384,512]{1,0:T(8,128)(2,1)S(1)}, bf16[384,512]{1,0:T(8,128)(2,1)S(1)}, u32[]{:S(2)}, u32[]{:S(2)}) %collective-permute-start.8) | collective-permute-done | bytes 393248 | tf_op jit(solution)/shard_map/ppermute | solution.py:313
  42.5 1.5 %collective-permute-start.12 = (bf16[16,1920]{1,0:T(8,128)(2,1)S(1)}, bf16[16,1920]{1,0:T(8,128)(2,1)S(1)}, u32[]{:S(2)}, u32[]{:S(2)}) collective-permute-start(bf16[16,1920]{1,0:T(8,128)(2,1)S(1)} %total.1.refs_0_), channel_id=1, source_target_pairs={{0,4},{4,0},{8,12},{12,8},{16,20},{20,16},{24,28},{28,24},{1,5},{5... | collective-permute-start | bytes 184328 | tf_op jit(solution)/shard_map/ppermute | solution.py:313
  44.4 2.6 %collective-permute-start.15 = (bf16[16,1920]{1,0:T(8,128)(2,1)S(1)}, bf16[16,1920]{1,0:T(8,128)(2,1)S(1)}, u32[]{:S(2)}, u32[]{:S(2)}) collective-permute-start(bf16[16,1920]{1,0:T(8,128)(2,1)S(1)} %total.1.refs_0_), channel_id=1, source_target_pairs={{0,16},{4,20},{8,24},{12,28},{16,0},{20,4},{24,8},{28,12},{1,17},{... | collective-permute-start | bytes 184328 | tf_op jit(solution)/shard_map/ppermute | solution.py:313
  47.8 0.6 collective-permute-start.17
  48.9 1.2 %collective-permute-start.14 = (bf16[16,1920]{1,0:T(8,128)(2,1)S(1)}, bf16[16,1920]{1,0:T(8,128)(2,1)S(1)}, u32[]{:S(2)}, u32[]{:S(2)}) collective-permute-start(bf16[16,1920]{1,0:T(8,128)(2,1)S(1)} %collective-permute-done.13.refs_2_), channel_id=1, source_target_pairs={{0,4},{4,0},{8,12},{12,8},{16,20},{20,16},{24,28},{28,24},{1,5},{5... | collective-permute-start | bytes 184328 | tf_op jit(solution)/shard_map/ppermute | solution.py:313
  50.0 0.9 %collective-permute-start.16 = (bf16[16,1920]{1,0:T(8,128)(2,1)S(1)}, bf16[16,1920]{1,0:T(8,128)(2,1)S(1)}, u32[]{:S(2)}, u32[]{:S(2)}) collective-permute-start(bf16[16,1920]{1,0:T(8,128)(2,1)S(1)} %collective-permute-done.15.refs_4_), channel_id=1, source_target_pairs={{0,4},{4,0},{8,12},{12,8},{16,20},{20,16},{24,28},{28,24},{1,5},{5... | collective-permute-start | bytes 184328 | tf_op jit(solution)/shard_map/ppermute | solution.py:313
  50.9 2.5 %collective-permute-done.14.refs_3_ = bf16[16,1920]{1,0:T(8,128)(2,1)S(1)} collective-permute-done((bf16[16,1920]{1,0:T(8,128)(2,1)S(1)}, bf16[16,1920]{1,0:T(8,128)(2,1)S(1)}, u32[]{:S(2)}, u32[]{:S(2)}) %collective-permute-start.14) | collective-permute-done | bytes 61472 | tf_op jit(solution)/shard_map/ppermute | solution.py:313
  53.4 0.8 %collective-permute-done.16.refs_5_ = bf16[16,1920]{1,0:T(8,128)(2,1)S(1)} collective-permute-done((bf16[16,1920]{1,0:T(8,128)(2,1)S(1)}, bf16[16,1920]{1,0:T(8,128)(2,1)S(1)}, u32[]{:S(2)}, u32[]{:S(2)}) %collective-permute-start.16) | collective-permute-done | bytes 61472 | tf_op jit(solution)/shard_map/ppermute | solution.py:313
  54.3 1.2 %scores.1 = (f32[128,512]{1,0:T(8,128)S(1)}, f32[128,1024]{1,0:T(8,128)S(1)}, f32[128,1024]{1,0:T(8,128)S(1)}, f32[128,1024]{1,0:T(8,128)S(1)}, f32[16,128]{1,0:T(8,128)S(1)}) custom-call(s32[1]{0:T(128)} %bitcast.1.me_ref, bf16[128,256]{1,0:T(8,128)(2,1)S(1)} %shard_map.128.three_pick_ref, bf16[128,256]{1,0:T(8,128)(2,1)S(1)} %shard_map.129.four_pick_ref, ...), custom_call_target="tpu_custom_call" | custom-call | flops 461373440 | bytes 3604480 | tf_op jit(solution)/shard_map/scores/pallas_call | solution.py:431
  55.4 0.9 %head_more.1.refs_1_ = f32[256,512]{1,0:T(8,128)S(1)} custom-call(s32[1]{0:T(128)} %bitcast.mine_ref, bf16[256,5120]{1,0:T(8,128)(2,1)S(1)} %copy-done.1, bf16[896,512]{1,0:T(8,128)(2,1)S(1)} %collective-permute-done.10.refs_0_, bf16[896,512]{1,0:T(8,128)(2,1)S(1)} %collective-permute-done.11.refs_1_, bf16[384,512]{1,0:T(8,128)(2,1)S(1)} %collective-permute-done.8.refs_2_, ...), custom_call_target="tpu_custom_call" | custom-call | flops 671088640 | bytes 2621440 | tf_op jit(solution)/shard_map/head_more/pallas_call | solution.py:412
  56.9 2.1 %collective-permute-start.18 = (f32[16,128]{1,0:T(8,128)S(1)}, f32[16,128]{1,0:T(8,128)S(1)}, u32[]{:S(2)}, u32[]{:S(2)}) collective-permute-start(f32[16,128]{1,0:T(8,128)S(1)} %broadcast_select_fusion), channel_id=1, source_target_pairs={{0,16},{4,20},{8,24},{12,28},{16,0},{20,4},{24,8},{28,12},{1,17},{... | collective-permute-start | bytes 24584 | tf_op jit(solution)/shard_map/ppermute | solution.py:313
  59.0 2.4 %collective-permute-done.18 = f32[16,128]{1,0:T(8,128)S(1)} collective-permute-done((f32[16,128]{1,0:T(8,128)S(1)}, f32[16,128]{1,0:T(8,128)S(1)}, u32[]{:S(2)}, u32[]{:S(2)}) %collective-permute-start.18) | collective-permute-done | bytes 8224 | tf_op jit(solution)/shard_map/ppermute | solution.py:313
  61.5 2.1 %collective-permute-start.19 = (f32[16,128]{1,0:T(8,128)S(1)}, f32[16,128]{1,0:T(8,128)S(1)}, u32[]{:S(2)}, u32[]{:S(2)}) collective-permute-start(f32[16,128]{1,0:T(8,128)S(1)} %pad_maximum_fusion), channel_id=1, source_target_pairs={{0,8},{4,12},{8,0},{12,4},{16,24},{20,28},{24,16},{28,20},{1,9},{5... | collective-permute-start | bytes 24584 | tf_op jit(solution)/shard_map/ppermute | solution.py:313
  63.6 1.7 %collective-permute-done.19 = f32[16,128]{1,0:T(8,128)S(1)} collective-permute-done((f32[16,128]{1,0:T(8,128)S(1)}, f32[16,128]{1,0:T(8,128)S(1)}, u32[]{:S(2)}, u32[]{:S(2)}) %collective-permute-start.19) | collective-permute-done | bytes 8224 | tf_op jit(solution)/shard_map/ppermute | solution.py:313
  65.2 1.0 %collective-permute-start.20 = (f32[16,128]{1,0:T(8,128)S(1)}, f32[16,128]{1,0:T(8,128)S(1)}, u32[]{:S(2)}, u32[]{:S(2)}) collective-permute-start(f32[16,128]{1,0:T(8,128)S(1)} %pad_maximum_fusion.1.own_ref), channel_id=1, source_target_pairs={{0,4},{4,0},{8,12},{12,8},{16,20},{20,16},{24,28},{28,24},{1,5},{5... | collective-permute-start | bytes 24584 | tf_op jit(solution)/shard_map/ppermute | solution.py:313
  66.2 2.7 %collective-permute-done.20.other_ref = f32[16,128]{1,0:T(8,128)S(1)} collective-permute-done((f32[16,128]{1,0:T(8,128)S(1)}, f32[16,128]{1,0:T(8,128)S(1)}, u32[]{:S(2)}, u32[]{:S(2)}) %collective-permute-start.20) | collective-permute-done | bytes 8224 | tf_op jit(solution)/shard_map/ppermute | solution.py:313
  68.9 1.7 %outputs.1 = (f32[256,512]{1,0:T(8,128)}, f32[128,512]{1,0:T(8,128)}, f32[128,1024]{1,0:T(8,128)}, f32[128,1024]{1,0:T(8,128)}, f32[128,1024]{1,0:T(8,128)}) custom-call(f32[16,128]{1,0:T(8,128)S(1)} %pad_maximum_fusion.1.own_ref, f32[16,128]{1,0:T(8,128)S(1)} %collective-permute-done.20.other_ref, s32[1,256]{1,0:T(1,128)S(1)} %bitcast.9, ...), custom_call_target="tpu_custom_call" | custom-call | flops 1048576 | bytes 8388608 | tf_op jit(solution)/shard_map/outputs/pallas_call | solution.py:452
  (37 shorter events, 3.0 us)
Async XLA Ops:
  0.6 18.7 %copy-start = (bf16[5120,4]{0,1:T(4,128)(2,1)S(1)}, bf16[5120,4]{0,1:T(4,128)(2,1)}, u32[]{:S(2)}) copy-start(bf16[5120,4]{0,1:T(4,128)(2,1)} %param.12) | copy-start | bytes 122884
  0.7 3.2 %copy-start.2 = (bf16[1280,512]{1,0:T(8,128)(2,1)S(1)}, bf16[1280,512]{1,0:T(8,128)(2,1)}, u32[]{:S(2)}) copy-start(bf16[1280,512]{1,0:T(8,128)(2,1)} %refs_0_) | copy-start | bytes 3932164
  0.7 18.7 %copy-start.1 = (bf16[256,5120]{1,0:T(8,128)(2,1)S(1)}, bf16[256,5120]{1,0:T(8,128)(2,1)}, u32[]{:S(2)}) copy-start(bf16[256,5120]{1,0:T(8,128)(2,1)} %tokens_ref.5) | copy-start | bytes 7864324
  3.9 16.3 %collective-permute-start.6 = (bf16[1280,512]{1,0:T(8,128)(2,1)S(1)}, bf16[1280,512]{1,0:T(8,128)(2,1)S(1)}, u32[]{:S(2)}, u32[]{:S(2)}) collective-permute-start(bf16[1280,512]{1,0:T(8,128)(2,1)S(1)} %copy-done.2), channel_id=1, source_target_pairs={{0,1},{1,0},{2,3},{3,2},{4,5},{5,4},{6,7},{7,6},{8,9},{9,8},{10,11... | collective-permute-start | bytes 3932168 | tf_op jit(solution)/shard_map/ppermute | solution.py:313
  4.4 13.3 %collective-permute-start = (f32[32,1920]{1,0:T(8,128)S(1)}, f32[32,1920]{1,0:T(8,128)S(1)}, u32[]{:S(2)}, u32[]{:S(2)}) collective-permute-start(f32[32,1920]{1,0:T(8,128)S(1)} %get-tuple-element.50), channel_id=1, source_target_pairs={{0,8},{4,12},{8,0},{12,4},{16,24},{20,28},{24,16},{28,20},{1,9},{5... | collective-permute-start | bytes 737288 | tf_op jit(solution)/shard_map/ppermute | solution.py:313
  7.1 6.2 %collective-permute-start.2 = (f32[16,1920]{1,0:T(8,128)S(1)}, f32[16,1920]{1,0:T(8,128)S(1)}, u32[]{:S(2)}, u32[]{:S(2)}) collective-permute-start(f32[16,1920]{1,0:T(8,128)S(1)} %get-tuple-element.54), channel_id=1, source_target_pairs={{0,4},{4,0},{8,12},{12,8},{16,20},{20,16},{24,28},{28,24},{1,5},{5... | collective-permute-start | bytes 368648 | tf_op jit(solution)/shard_map/ppermute | solution.py:313
  8.6 7.2 %collective-permute-start.4 = (f32[16,1920]{1,0:T(8,128)S(1)}, f32[16,1920]{1,0:T(8,128)S(1)}, u32[]{:S(2)}, u32[]{:S(2)}) collective-permute-start(f32[16,1920]{1,0:T(8,128)S(1)} %get-tuple-element.56), channel_id=1, source_target_pairs={{0,4},{4,0},{8,12},{12,8},{16,20},{20,16},{24,28},{28,24},{1,5},{5... | collective-permute-start | bytes 368648 | tf_op jit(solution)/shard_map/ppermute | solution.py:313
  9.1 21.8 %collective-permute-start.10 = (bf16[896,512]{1,0:T(8,128)(2,1)S(1)}, bf16[896,512]{1,0:T(8,128)(2,1)S(1)}, u32[]{:S(2)}, u32[]{:S(2)}) collective-permute-start(bf16[896,512]{1,0:T(8,128)(2,1)S(1)} %get-tuple-element.66), channel_id=1, source_target_pairs={{0,2},{1,3},{2,0},{3,1},{4,6},{5,7},{6,4},{7,5},{8,10},{9,11},{10,... | collective-permute-start | bytes 2752520 | tf_op jit(solution)/shard_map/ppermute | solution.py:313
  13.3 9.0 %collective-permute-start.3 = (f32[16,1920]{1,0:T(8,128)S(1)}, f32[16,1920]{1,0:T(8,128)S(1)}, u32[]{:S(2)}, u32[]{:S(2)}) collective-permute-start(f32[16,1920]{1,0:T(8,128)S(1)} %add.16), channel_id=1, source_target_pairs={{0,24},{4,28},{8,16},{12,20},{16,8},{20,12},{24,0},{28,4},{1,25},{... | collective-permute-start | bytes 368648 | tf_op jit(solution)/shard_map/ppermute | solution.py:313
  15.8 10.0 %collective-permute-start.5 = (f32[16,1920]{1,0:T(8,128)S(1)}, f32[16,1920]{1,0:T(8,128)S(1)}, u32[]{:S(2)}, u32[]{:S(2)}) collective-permute-start(f32[16,1920]{1,0:T(8,128)S(1)} %add.17), channel_id=1, source_target_pairs={{0,16},{4,20},{8,24},{12,28},{16,0},{20,4},{24,8},{28,12},{1,17},{... | collective-permute-start | bytes 368648 | tf_op jit(solution)/shard_map/ppermute | solution.py:313
  17.8 8.0 %collective-permute-start.1 = (f32[16,1920]{1,0:T(8,128)S(1)}, f32[16,1920]{1,0:T(8,128)S(1)}, u32[]{:S(2)}, u32[]{:S(2)}) collective-permute-start(f32[16,1920]{1,0:T(8,128)S(1)} %slice_add_fusion), channel_id=1, source_target_pairs={{0,4},{4,0},{8,12},{12,8},{16,20},{20,16},{24,28},{28,24},{1,5},{5... | collective-permute-start | bytes 368648 | tf_op jit(solution)/shard_map/ppermute | solution.py:313
  20.1 26.9 %copy-start.3 = (s32[256,1]{0,1:T(1,128)S(1)}, s32[256,1]{0,1:T(1,128)}, u32[]{:S(2)}) copy-start(s32[256,1]{0,1:T(1,128)} %param.10) | copy-start | bytes 3076
  30.9 24.5 %collective-permute-start.11 = (bf16[896,512]{1,0:T(8,128)(2,1)S(1)}, bf16[896,512]{1,0:T(8,128)(2,1)S(1)}, u32[]{:S(2)}, u32[]{:S(2)}) collective-permute-start(bf16[896,512]{1,0:T(8,128)(2,1)S(1)} %collective-permute-done.10.refs_0_), channel_id=1, source_target_pairs={{0,1},{1,0},{2,3},{3,2},{4,5},{5,4},{6,7},{7,6},{8,9},{9,8},{10,11... | collective-permute-start | bytes 2752520 | tf_op jit(solution)/shard_map/ppermute | solution.py:313
  30.9 11.5 %collective-permute-start.8 = (bf16[384,512]{1,0:T(8,128)(2,1)S(1)}, bf16[384,512]{1,0:T(8,128)(2,1)S(1)}, u32[]{:S(2)}, u32[]{:S(2)}) collective-permute-start(bf16[384,512]{1,0:T(8,128)(2,1)S(1)} %get-tuple-element.64), channel_id=1, source_target_pairs={{0,2},{1,3},{2,0},{3,1},{4,6},{5,7},{6,4},{7,5},{8,10},{9,11},{10,... | collective-permute-start | bytes 1179656 | tf_op jit(solution)/shard_map/ppermute | solution.py:313
  32.4 10.0 %collective-permute-start.7 = (bf16[16,1920]{1,0:T(8,128)(2,1)S(1)}, bf16[16,1920]{1,0:T(8,128)(2,1)S(1)}, u32[]{:S(2)}, u32[]{:S(2)}) collective-permute-start(bf16[16,1920]{1,0:T(8,128)(2,1)S(1)} %total.1.refs_0_), channel_id=1, source_target_pairs={{0,24},{4,28},{8,16},{12,20},{16,8},{20,12},{24,0},{28,4},{1,25},{... | collective-permute-start | bytes 184328 | tf_op jit(solution)/shard_map/ppermute | solution.py:313
  42.5 13.8 %collective-permute-start.9 = (bf16[384,512]{1,0:T(8,128)(2,1)S(1)}, bf16[384,512]{1,0:T(8,128)(2,1)S(1)}, u32[]{:S(2)}, u32[]{:S(2)}) collective-permute-start(bf16[384,512]{1,0:T(8,128)(2,1)S(1)} %collective-permute-done.8.refs_2_), channel_id=1, source_target_pairs={{0,1},{1,0},{2,3},{3,2},{4,5},{5,4},{6,7},{7,6},{8,9},{9,8},{10,11... | collective-permute-start | bytes 1179656 | tf_op jit(solution)/shard_map/ppermute | solution.py:313
  42.5 5.3 %collective-permute-start.12 = (bf16[16,1920]{1,0:T(8,128)(2,1)S(1)}, bf16[16,1920]{1,0:T(8,128)(2,1)S(1)}, u32[]{:S(2)}, u32[]{:S(2)}) collective-permute-start(bf16[16,1920]{1,0:T(8,128)(2,1)S(1)} %total.1.refs_0_), channel_id=1, source_target_pairs={{0,4},{4,0},{8,12},{12,8},{16,20},{20,16},{24,28},{28,24},{1,5},{5... | collective-permute-start | bytes 184328 | tf_op jit(solution)/shard_map/ppermute | solution.py:313
  44.0 4.9 %collective-permute-start.13 = (bf16[16,1920]{1,0:T(8,128)(2,1)S(1)}, bf16[16,1920]{1,0:T(8,128)(2,1)S(1)}, u32[]{:S(2)}, u32[]{:S(2)}) collective-permute-start(bf16[16,1920]{1,0:T(8,128)(2,1)S(1)} %total.1.refs_0_), channel_id=1, source_target_pairs={{0,8},{4,12},{8,0},{12,4},{16,24},{20,28},{24,16},{28,20},{1,9},{5... | collective-permute-start | bytes 184328 | tf_op jit(solution)/shard_map/ppermute | solution.py:313
  44.4 5.6 %collective-permute-start.15 = (bf16[16,1920]{1,0:T(8,128)(2,1)S(1)}, bf16[16,1920]{1,0:T(8,128)(2,1)S(1)}, u32[]{:S(2)}, u32[]{:S(2)}) collective-permute-start(bf16[16,1920]{1,0:T(8,128)(2,1)S(1)} %total.1.refs_0_), channel_id=1, source_target_pairs={{0,16},{4,20},{8,24},{12,28},{16,0},{20,4},{24,8},{28,12},{1,17},{... | collective-permute-start | bytes 184328 | tf_op jit(solution)/shard_map/ppermute | solution.py:313
  47.8 6.5 %collective-permute-start.17 = (bf16[16,1920]{1,0:T(8,128)(2,1)S(1)}, bf16[16,1920]{1,0:T(8,128)(2,1)S(1)}, u32[]{:S(2)}, u32[]{:S(2)}) collective-permute-start(bf16[16,1920]{1,0:T(8,128)(2,1)S(1)} %collective-permute-done.7.refs_6_), channel_id=1, source_target_pairs={{0,4},{4,0},{8,12},{12,8},{16,20},{20,16},{24,28},{28,24},{1,5},{5... | collective-permute-start | bytes 184328 | tf_op jit(solution)/shard_map/ppermute | solution.py:313
  48.9 4.6 %collective-permute-start.14 = (bf16[16,1920]{1,0:T(8,128)(2,1)S(1)}, bf16[16,1920]{1,0:T(8,128)(2,1)S(1)}, u32[]{:S(2)}, u32[]{:S(2)}) collective-permute-start(bf16[16,1920]{1,0:T(8,128)(2,1)S(1)} %collective-permute-done.13.refs_2_), channel_id=1, source_target_pairs={{0,4},{4,0},{8,12},{12,8},{16,20},{20,16},{24,28},{28,24},{1,5},{5... | collective-permute-start | bytes 184328 | tf_op jit(solution)/shard_map/ppermute | solution.py:313
  50.0 4.2 %collective-permute-start.16 = (bf16[16,1920]{1,0:T(8,128)(2,1)S(1)}, bf16[16,1920]{1,0:T(8,128)(2,1)S(1)}, u32[]{:S(2)}, u32[]{:S(2)}) collective-permute-start(bf16[16,1920]{1,0:T(8,128)(2,1)S(1)} %collective-permute-done.15.refs_4_), channel_id=1, source_target_pairs={{0,4},{4,0},{8,12},{12,8},{16,20},{20,16},{24,28},{28,24},{1,5},{5... | collective-permute-start | bytes 184328 | tf_op jit(solution)/shard_map/ppermute | solution.py:313
  56.9 4.6 %collective-permute-start.18 = (f32[16,128]{1,0:T(8,128)S(1)}, f32[16,128]{1,0:T(8,128)S(1)}, u32[]{:S(2)}, u32[]{:S(2)}) collective-permute-start(f32[16,128]{1,0:T(8,128)S(1)} %broadcast_select_fusion), channel_id=1, source_target_pairs={{0,16},{4,20},{8,24},{12,28},{16,0},{20,4},{24,8},{28,12},{1,17},{... | collective-permute-start | bytes 24584 | tf_op jit(solution)/shard_map/ppermute | solution.py:313
  61.5 3.7 %collective-permute-start.19 = (f32[16,128]{1,0:T(8,128)S(1)}, f32[16,128]{1,0:T(8,128)S(1)}, u32[]{:S(2)}, u32[]{:S(2)}) collective-permute-start(f32[16,128]{1,0:T(8,128)S(1)} %pad_maximum_fusion), channel_id=1, source_target_pairs={{0,8},{4,12},{8,0},{12,4},{16,24},{20,28},{24,16},{28,20},{1,9},{5... | collective-permute-start | bytes 24584 | tf_op jit(solution)/shard_map/ppermute | solution.py:313
  65.2 3.7 %collective-permute-start.20 = (f32[16,128]{1,0:T(8,128)S(1)}, f32[16,128]{1,0:T(8,128)S(1)}, u32[]{:S(2)}, u32[]{:S(2)}) collective-permute-start(f32[16,128]{1,0:T(8,128)S(1)} %pad_maximum_fusion.1.own_ref), channel_id=1, source_target_pairs={{0,4},{4,0},{8,12},{12,8},{16,20},{20,16},{24,28},{28,24},{1,5},{5... | collective-permute-start | bytes 24584 | tf_op jit(solution)/shard_map/ppermute | solution.py:313
